TPU v7x, 768 devices: a whole 4x8x12 slice. The times are simulated.
768 devices in a mesh: gx: 96 (over y, z_hi, x), gy: 8 (over z_lo, core).
Axes of the slice: x: 4, y: 8, z: 12 (z_hi: 3, z_lo: 4; z = z_hi * 4 + z_lo), core: 2. Of those that a mesh axis runs over, the one named last changes fastest.
Arguments:
- u_now_c: float32 [3, 192, 32, 128], P(None, 'gx', 'gy'), may hold values from -6 to 6
- u_prev_c: float32 [3, 192, 32, 128], P(None, 'gx', 'gy'), may hold values from -6 to 6
- memory_c: float32 [3, 3, 192, 32, 128], P(None, None, 'gx', 'gy'), may hold values from -3 to 3
- mu_c: float32 [192, 32, 128], P('gx', 'gy'), may hold values from 0.5 to 1.5
- lam_c: float32 [192, 32, 128], P('gx', 'gy'), may hold values from 0.5 to 1.5
- rho_c: float32 [192, 32, 128], P('gx', 'gy'), may hold values from 1 to 2
- q_c: float32 [3, 192, 32, 128], P(None, 'gx', 'gy'), may hold values from 0.05 to 0.4
- omega_c: float32 [3, 192, 32, 128], P(None, 'gx', 'gy'), may hold values from 0.1 to 8
- u_now_f: float32 [3, 384, 64, 128], P(None, 'gx', 'gy'), may hold values from -6 to 6
- u_prev_f: float32 [3, 384, 64, 128], P(None, 'gx', 'gy'), may hold values from -6 to 6
- memory_f: float32 [3, 3, 384, 64, 128], P(None, None, 'gx', 'gy'), may hold values from -3 to 3
- mu_f: float32 [384, 64, 128], P('gx', 'gy'), may hold values from 0.5 to 1.5
- lam_f: float32 [384, 64, 128], P('gx', 'gy'), may hold values from 0.5 to 1.5
- rho_f: float32 [384, 64, 128], P('gx', 'gy'), may hold values from 1 to 2
- q_f: float32 [3, 384, 64, 128], P(None, 'gx', 'gy'), may hold values from 0.05 to 0.4
- omega_f: float32 [3, 384, 64, 128], P(None, 'gx', 'gy'), may hold values from 0.1 to 8
- stretch_f: float32 [384, 64], P('gx', 'gy'), may hold values from 0.35 to 0.7
Outputs:
- u_out_c: float32 [3, 192, 32, 128], P(None, 'gx', 'gy')
- u_out_f: float32 [3, 384, 64, 128], P(None, 'gx', 'gy')
- memory_out_c: float32 [3, 3, 192, 32, 128], P(None, None, 'gx', 'gy')
- memory_out_f: float32 [3, 3, 384, 64, 128], P(None, None, 'gx', 'gy')
All inputs are finite; a program needn't handle non-finite values.
Results may differ from a plain program's by a relative error of at most 0.0001.
Values sent between devices are 32-bit elements; how exact they have to be, the bound alone decides.
No kernel may reach another device: no remote copies, remote signals or barrier semaphores. Data moves between devices by JAX's collectives and lax.ppermute only.
A program may use at most 32 MiB of HBM per device.

v0:
```python
import jax
import jax.numpy as jnp
from jax import lax
from jax.sharding import PartitionSpec as P

STEPS = 2


DT = 0.1


def padded_2(cells, sides, width):
    for axis, dim in sides:
        count = lax.axis_size(axis)
        ends = count - 1
        head = lax.slice_in_dim(cells, 0, width, axis=dim)
        tail = lax.slice_in_dim(cells, cells.shape[dim] - width, cells.shape[dim], axis=dim)
        cells = jnp.concatenate(
            [
                lax.ppermute(tail, axis, [(i, (i + 1) % count) for i in range(ends)]),
                cells,
                lax.ppermute(head, axis, [((i + 1) % count, i) for i in range(ends)]),
            ],
            axis=dim,
        )
    return cells


def restrict(plane):
    comps, wide, tall = plane.shape
    return plane.reshape(comps, wide // 2, 2, tall // 2, 2).mean(axis=(2, 4))


def prolong(plane):
    comps = plane.shape[0]
    even = 0.75 * plane[:, 1:-1] + 0.25 * plane[:, :-2]
    odd = 0.75 * plane[:, 1:-1] + 0.25 * plane[:, 2:]
    rows = jnp.stack([even, odd], axis=2).reshape(comps, -1, plane.shape[2])
    even = 0.75 * rows[:, :, 1:-1] + 0.25 * rows[:, :, :-2]
    odd = 0.75 * rows[:, :, 1:-1] + 0.25 * rows[:, :, 2:]
    return jnp.stack([even, odd], axis=3).reshape(comps, rows.shape[1], -1)


def coarse_extend(field_c, fine_plane):
    top = restrict(fine_plane)[..., None]
    return jnp.concatenate([top, field_c, jnp.zeros_like(top)], axis=3)


def shifted(padded, offx, offy, offz):
    sizes = padded.shape
    return padded[
        :,
        1 + offx : sizes[1] - 1 + offx,
        1 + offy : sizes[2] - 1 + offy,
        1 + offz : sizes[3] - 1 + offz,
    ]


def mixed(padded, comp, first, second):
    plus_plus = [0, 0, 0]
    plus_plus[first] = 1
    plus_plus[second] = 1
    plus_minus = [0, 0, 0]
    plus_minus[first] = 1
    plus_minus[second] = -1
    minus_plus = [0, 0, 0]
    minus_plus[first] = -1
    minus_plus[second] = 1
    minus_minus = [0, 0, 0]
    minus_minus[first] = -1
    minus_minus[second] = -1
    total = shifted(padded[comp : comp + 1], *plus_plus) - shifted(
        padded[comp : comp + 1], *plus_minus
    )
    total = (
        total
        - shifted(padded[comp : comp + 1], *minus_plus)
        + shifted(padded[comp : comp + 1], *minus_minus)
    )
    return total[0]


def operator(padded, shear, lame, level_h, level_hz):
    across = level_h * level_h
    vertical = level_hz * level_hz
    center = shifted(padded, 0, 0, 0)
    dxx = (shifted(padded, 1, 0, 0) + shifted(padded, -1, 0, 0) - 2.0 * center) / across
    dyy = (shifted(padded, 0, 1, 0) + shifted(padded, 0, -1, 0) - 2.0 * center) / across
    dzz = (shifted(padded, 0, 0, 1) + shifted(padded, 0, 0, -1) - 2.0 * center) / vertical
    flat = 4.0 * across
    slant = 4.0 * level_h * level_hz
    grad_x = dxx[0] + mixed(padded, 1, 0, 1) / flat + mixed(padded, 2, 0, 2) / slant
    grad_y = mixed(padded, 0, 0, 1) / flat + dyy[1] + mixed(padded, 2, 1, 2) / slant
    grad_z = mixed(padded, 0, 0, 2) / slant + mixed(padded, 1, 1, 2) / slant + dzz[2]
    return shear * (dxx + dyy + dzz) + (lame + shear) * jnp.stack([grad_x, grad_y, grad_z])


def edge_keep(count, where_now, total):
    places = jnp.arange(count)
    low = jnp.logical_and(places == 0, where_now == 0)
    high = jnp.logical_and(places == count - 1, where_now == total - 1)
    return jnp.where(jnp.logical_or(low, high), 0.0, 1.0).astype(jnp.float32)


def both_levels(field_c, field_f):
    extended_c = coarse_extend(field_c, field_f[..., -1])
    comps, wide, tall, depth = field_f.shape
    topped = jnp.concatenate([field_f[..., :1], field_f], axis=3)
    folded = topped.reshape(comps, wide // 2, 2, tall // 2, 2, depth + 1)
    folded = folded.transpose(0, 1, 3, 2, 4, 5).reshape(
        comps, wide // 2, tall // 2, 4 * (depth + 1)
    )
    joined = jnp.concatenate([extended_c, folded], axis=3)
    padded = padded_2(joined, (("gx", 1), ("gy", 2)), 1)
    split = extended_c.shape[3]
    full_c = padded[..., :split]
    unfolded = padded[..., split:].reshape(comps, wide // 2 + 2, tall // 2 + 2, 2, 2, depth + 1)
    unfolded = unfolded.transpose(0, 1, 3, 2, 4, 5).reshape(comps, wide + 4, tall + 4, depth + 1)
    fine_cols = unfolded[:, 1:-1, 1:-1]
    plane = jnp.pad(full_c[..., 1], ((0, 0), (1, 1), (1, 1)))
    bottom = prolong(plane)[:, 1:-1, 1:-1]
    keep_x = edge_keep(wide + 2, lax.axis_index("gx"), lax.axis_size("gx"))
    keep_y = edge_keep(tall + 2, lax.axis_index("gy"), lax.axis_size("gy"))
    keep = keep_x[:, None] * keep_y[None, :]
    bottom = bottom * keep[None]
    full_f = jnp.concatenate([fine_cols, bottom[..., None]], axis=3)
    return (full_c, full_f)


def shards(
    u_now_c,
    u_prev_c,
    memory_c,
    mu_c,
    lam_c,
    rho_c,
    q_c,
    omega_c,
    u_now_f,
    u_prev_f,
    memory_f,
    mu_f,
    lam_f,
    rho_f,
    q_f,
    omega_f,
    stretch_f,
):
    height_f = stretch_f[:, :, None]
    for step in range(STEPS):
        weighted_c = q_c[:, None] * memory_c
        weighted_f = q_f[:, None] * memory_f
        net_c = u_now_c - jnp.sum(weighted_c, axis=0)
        net_f = u_now_f - jnp.sum(weighted_f, axis=0)
        full_c, full_f = both_levels(net_c, net_f)
        force_c = operator(full_c, mu_c, lam_c, 1.0, 1.0)
        force_f = operator(full_f, mu_f, lam_f, 0.5, height_f)
        next_c = 2.0 * u_now_c - u_prev_c + DT * DT / rho_c * force_c
        next_f = 2.0 * u_now_f - u_prev_f + DT * DT / rho_f * force_f
        memory_c = memory_c + DT * omega_c[:, None] * (u_now_c[None] - memory_c)
        memory_f = memory_f + DT * omega_f[:, None] * (u_now_f[None] - memory_f)
        u_prev_c, u_now_c = (u_now_c, next_c)
        u_prev_f, u_now_f = (u_now_f, next_f)
    return (u_now_c, u_now_f, memory_c, memory_f)


def solution(mesh):
    return jax.shard_map(
        shards,
        mesh=mesh,
        in_specs=(
            P(None, "gx", "gy", None),
            P(None, "gx", "gy", None),
            P(None, None, "gx", "gy", None),
            P("gx", "gy", None),
            P("gx", "gy", None),
            P("gx", "gy", None),
            P(None, "gx", "gy", None),
            P(None, "gx", "gy", None),
            P(None, "gx", "gy", None),
            P(None, "gx", "gy", None),
            P(None, None, "gx", "gy", None),
            P("gx", "gy", None),
            P("gx", "gy", None),
            P("gx", "gy", None),
            P(None, "gx", "gy", None),
            P(None, "gx", "gy", None),
            P("gx", "gy"),
        ),
        out_specs=(
            P(None, "gx", "gy", None),
            P(None, "gx", "gy", None),
            P(None, None, "gx", "gy", None),
            P(None, None, "gx", "gy", None),
        ),
        check_vma=False,
    )
```

profile of v0, /device:TPU:33, one launch (start us, length us, event | category | flops | bytes accessed | tf_op | source)
XLA Modules:
  0.0 76.3 jit_solution(1754897446636510565)
XLA Ops:
  0.7 0.8 %broadcast_multiply_fusion = f32[3,4,8,128]{3,2,1,0:T(8,128)S(1)} fusion(f32[3,4,8,128]{3,2,1,0:T(8,128)} %param.32), kind=kLoop, calls=%fused_computation.140 | loop fusion | flops 12288 | bytes 98304 | tf_op jit(solution)/shard_map/mul | solution.py:161
  1.5 1.0 %multiply_reduce_fusion = (f32[3,4,8,128]{3,2,1,0:T(8,128)S(1)}, f32[3,4,8,128]{3,2,1,0:T(8,128)S(1)}) fusion(f32[3,3,4,8,128]{4,3,2,1,0:T(8,128)} %param.27, f32[3,4,8,128]{3,2,1,0:T(8,128)S(1)} %copy-done, f32[3,4,8,128]{3,2,1,0:T(8,128)S(1)} %broadcast_multiply_fusion, f32[3,4,8,128]{3,2,1,0:T(8,128)S(1)} %copy-done.5), kind=kLoop, calls=%fused_computation.77 | loop fusion | flops 233472 | bytes 393216 | tf_op jit(solution)/shard_map/reduce_sum | solution.py:154
  3.0 0.5 copy-done.11
  3.6 0.6 copy-done.2
  4.8 16.4 %collective-permute-start = (f32[3,1,4,646]{3,2,1,0:T(4,128)S(1)}, f32[3,1,4,646]{3,2,1,0:T(4,128)S(1)}, u32[]{:S(2)}, u32[]{:S(2)}) collective-permute-start(f32[3,1,4,646]{3,2,1,0:T(4,128)S(1)} %get-tuple-element.49), channel_id=1, source_target_pairs={{8,0},{16,8},{24,16},{32,24},{40,32},{48,40},{56,48},{64,56},{72,6... | collective-permute-start | bytes 93032 | tf_op jit(solution)/shard_map/ppermute | solution.py:22
  21.2 1.9 %collective-permute-start.1 = (f32[3,1,4,646]{3,2,1,0:T(4,128)S(1)}, f32[3,1,4,646]{3,2,1,0:T(4,128)S(1)}, u32[]{:S(2)}, u32[]{:S(2)}) collective-permute-start(f32[3,1,4,646]{3,2,1,0:T(4,128)S(1)} %get-tuple-element.48), channel_id=1, source_target_pairs={{0,8},{8,16},{16,24},{24,32},{32,40},{40,48},{48,56},{56,64},{64,7... | collective-permute-start | bytes 93032 | tf_op jit(solution)/shard_map/ppermute | solution.py:20
  23.2 0.7 copy-done.14
  23.9 0.6 copy-done.15
  24.6 0.7 copy-done.7
  25.2 10.3 %collective-permute-done.1 = f32[3,1,4,646]{3,2,1,0:T(4,128)S(1)} collective-permute-done((f32[3,1,4,646]{3,2,1,0:T(4,128)S(1)}, f32[3,1,4,646]{3,2,1,0:T(4,128)S(1)}, u32[]{:S(2)}, u32[]{:S(2)}) %collective-permute-start.1) | collective-permute-done | bytes 31040 | tf_op jit(solution)/shard_map/ppermute | solution.py:20
  35.8 2.7 %collective-permute-start.2 = (f32[3,4,1,646]{3,2,1,0:T(1,128)S(1)}, f32[3,4,1,646]{3,2,1,0:T(1,128)S(1)}, u32[]{:S(2)}, u32[]{:S(2)}) collective-permute-start(f32[3,4,1,646]{3,2,1,0:T(1,128)S(1)} %get-tuple-element.40), channel_id=1, source_target_pairs={{1,0},{2,1},{3,2},{4,3},{5,4},{6,5},{7,6},{9,8},{10,9},{11,10},{12... | collective-permute-start | bytes 93032 | tf_op jit(solution)/shard_map/ppermute | solution.py:22
  38.4 3.7 %collective-permute-start.3 = (f32[3,4,1,646]{3,2,1,0:T(1,128)S(1)}, f32[3,4,1,646]{3,2,1,0:T(1,128)S(1)}, u32[]{:S(2)}, u32[]{:S(2)}) collective-permute-start(f32[3,4,1,646]{3,2,1,0:T(1,128)S(1)} %get-tuple-element.41), channel_id=1, source_target_pairs={{0,1},{1,2},{2,3},{3,4},{4,5},{5,6},{6,7},{8,9},{9,10},{10,11},{11... | collective-permute-start | bytes 93032 | tf_op jit(solution)/shard_map/ppermute | solution.py:20
  42.3 0.8 %collective-permute-done.3 = f32[3,4,1,646]{3,2,1,0:T(1,128)S(1)} collective-permute-done((f32[3,4,1,646]{3,2,1,0:T(1,128)S(1)}, f32[3,4,1,646]{3,2,1,0:T(1,128)S(1)}, u32[]{:S(2)}, u32[]{:S(2)}) %collective-permute-start.3) | collective-permute-done | bytes 31040 | tf_op jit(solution)/shard_map/ppermute | solution.py:20
  43.6 0.5 reshape.132
  44.2 0.2 reshape.142
  44.9 0.4 copy.102
  45.8 0.6 copy-done.6
  47.8 0.6 copy-done.12
  48.6 1.9 %collective-permute-start.4 = (f32[3,1,4,646]{3,2,1,0:T(4,128)S(1)}, f32[3,1,4,646]{3,2,1,0:T(4,128)S(1)}, u32[]{:S(2)}, u32[]{:S(2)}) collective-permute-start(f32[3,1,4,646]{3,2,1,0:T(4,128)S(1)} %get-tuple-element.47), channel_id=1, source_target_pairs={{8,0},{16,8},{24,16},{32,24},{40,32},{48,40},{56,48},{64,56},{72,6... | collective-permute-start | bytes 93032 | tf_op jit(solution)/shard_map/ppermute | solution.py:22
  50.5 3.4 %collective-permute-start.5 = (f32[3,1,4,646]{3,2,1,0:T(4,128)S(1)}, f32[3,1,4,646]{3,2,1,0:T(4,128)S(1)}, u32[]{:S(2)}, u32[]{:S(2)}) collective-permute-start(f32[3,1,4,646]{3,2,1,0:T(4,128)S(1)} %get-tuple-element.46), channel_id=1, source_target_pairs={{0,8},{8,16},{16,24},{24,32},{32,40},{40,48},{48,56},{56,64},{64,7... | collective-permute-start | bytes 93032 | tf_op jit(solution)/shard_map/ppermute | solution.py:20
  53.9 0.7 multiply_add_fusion
  54.6 0.6 multiply_add_fusion.2
  55.2 8.2 %collective-permute-done.5 = f32[3,1,4,646]{3,2,1,0:T(4,128)S(1)} collective-permute-done((f32[3,1,4,646]{3,2,1,0:T(4,128)S(1)}, f32[3,1,4,646]{3,2,1,0:T(4,128)S(1)}, u32[]{:S(2)}, u32[]{:S(2)}) %collective-permute-start.5) | collective-permute-done | bytes 31040 | tf_op jit(solution)/shard_map/ppermute | solution.py:20
  63.7 1.9 %collective-permute-start.6 = (f32[3,4,1,646]{3,2,1,0:T(1,128)S(1)}, f32[3,4,1,646]{3,2,1,0:T(1,128)S(1)}, u32[]{:S(2)}, u32[]{:S(2)}) collective-permute-start(f32[3,4,1,646]{3,2,1,0:T(1,128)S(1)} %get-tuple-element.38), channel_id=1, source_target_pairs={{1,0},{2,1},{3,2},{4,3},{5,4},{6,5},{7,6},{9,8},{10,9},{11,10},{12... | collective-permute-start | bytes 93032 | tf_op jit(solution)/shard_map/ppermute | solution.py:22
  65.6 5.3 %collective-permute-start.7 = (f32[3,4,1,646]{3,2,1,0:T(1,128)S(1)}, f32[3,4,1,646]{3,2,1,0:T(1,128)S(1)}, u32[]{:S(2)}, u32[]{:S(2)}) collective-permute-start(f32[3,4,1,646]{3,2,1,0:T(1,128)S(1)} %get-tuple-element.39), channel_id=1, source_target_pairs={{0,1},{1,2},{2,3},{3,4},{4,5},{5,6},{6,7},{8,9},{9,10},{10,11},{11... | collective-permute-start | bytes 93032 | tf_op jit(solution)/shard_map/ppermute | solution.py:20
  71.1 0.8 %collective-permute-done.7 = f32[3,4,1,646]{3,2,1,0:T(1,128)S(1)} collective-permute-done((f32[3,4,1,646]{3,2,1,0:T(1,128)S(1)}, f32[3,4,1,646]{3,2,1,0:T(1,128)S(1)}, u32[]{:S(2)}, u32[]{:S(2)}) %collective-permute-start.7) | collective-permute-done | bytes 31040 | tf_op jit(solution)/shard_map/ppermute | solution.py:20
  72.3 0.2 fusion.25
  72.8 0.5 reshape.138
  73.4 0.2 reshape.143
  74.0 0.4 copy.134
  75.0 0.6 fusion.133
  75.7 0.7 fusion.63
  (113 shorter events, 6.7 us)
Async XLA Ops:
  0.6 0.9 %copy-start = (f32[3,4,8,128]{3,2,1,0:T(8,128)S(1)}, f32[3,4,8,128]{3,2,1,0:T(8,128)}, u32[]{:S(2)}) copy-start(f32[3,4,8,128]{3,2,1,0:T(8,128)} %param.25) | copy-start | bytes 147460
  0.6 0.8 %copy-start.5 = (f32[3,4,8,128]{3,2,1,0:T(8,128)S(1)}, f32[3,4,8,128]{3,2,1,0:T(8,128)}, u32[]{:S(2)}) copy-start(f32[3,4,8,128]{3,2,1,0:T(8,128)} %param.31) | copy-start | bytes 147460
  2.8 0.7 copy-start.11
  2.8 0.8 %copy-start.3 = (f32[3,3,2,4,128]{4,3,2,1,0:T(4,128)S(1)}, f32[3,3,2,4,128]{4,3,2,1,0:T(4,128)}, u32[]{:S(2)}) copy-start(f32[3,3,2,4,128]{4,3,2,1,0:T(4,128)} %param.19) | copy-start | bytes 110596
  3.5 0.7 copy-start.2
  3.5 0.7 copy-start.10
  4.8 18.3 %copy-start.9 = (f32[4,8,128]{2,1,0:T(8,128)S(1)}, f32[4,8,128]{2,1,0:T(8,128)}, u32[]{:S(2)}) copy-start(f32[4,8,128]{2,1,0:T(8,128)} %param.30) | copy-start | bytes 49156
  4.8 20.4 %collective-permute-start = (f32[3,1,4,646]{3,2,1,0:T(4,128)S(1)}, f32[3,1,4,646]{3,2,1,0:T(4,128)S(1)}, u32[]{:S(2)}, u32[]{:S(2)}) collective-permute-start(f32[3,1,4,646]{3,2,1,0:T(4,128)S(1)} %get-tuple-element.49), channel_id=1, source_target_pairs={{8,0},{16,8},{24,16},{32,24},{40,32},{48,40},{56,48},{64,56},{72,6... | collective-permute-start | bytes 93032 | tf_op jit(solution)/shard_map/ppermute | solution.py:22
  21.2 14.4 %collective-permute-start.1 = (f32[3,1,4,646]{3,2,1,0:T(4,128)S(1)}, f32[3,1,4,646]{3,2,1,0:T(4,128)S(1)}, u32[]{:S(2)}, u32[]{:S(2)}) collective-permute-start(f32[3,1,4,646]{3,2,1,0:T(4,128)S(1)} %get-tuple-element.48), channel_id=1, source_target_pairs={{0,8},{8,16},{16,24},{24,32},{32,40},{40,48},{48,56},{56,64},{64,7... | collective-permute-start | bytes 93032 | tf_op jit(solution)/shard_map/ppermute | solution.py:20
  23.1 0.7 copy-start.14
  23.1 1.4 %copy-start.8 = (f32[4,8,128]{2,1,0:T(8,128)S(1)}, f32[4,8,128]{2,1,0:T(8,128)}, u32[]{:S(2)}) copy-start(f32[4,8,128]{2,1,0:T(8,128)} %param.29) | copy-start | bytes 49156
  23.8 0.7 copy-start.4
  23.8 0.7 copy-start.15
  24.5 0.7 copy-start.7
  24.5 0.7 copy-start.13
  35.8 6.5 %collective-permute-start.2 = (f32[3,4,1,646]{3,2,1,0:T(1,128)S(1)}, f32[3,4,1,646]{3,2,1,0:T(1,128)S(1)}, u32[]{:S(2)}, u32[]{:S(2)}) collective-permute-start(f32[3,4,1,646]{3,2,1,0:T(1,128)S(1)} %get-tuple-element.40), channel_id=1, source_target_pairs={{1,0},{2,1},{3,2},{4,3},{5,4},{6,5},{7,6},{9,8},{10,9},{11,10},{12... | collective-permute-start | bytes 93032 | tf_op jit(solution)/shard_map/ppermute | solution.py:22
  38.4 4.7 %collective-permute-start.3 = (f32[3,4,1,646]{3,2,1,0:T(1,128)S(1)}, f32[3,4,1,646]{3,2,1,0:T(1,128)S(1)}, u32[]{:S(2)}, u32[]{:S(2)}) collective-permute-start(f32[3,4,1,646]{3,2,1,0:T(1,128)S(1)} %get-tuple-element.41), channel_id=1, source_target_pairs={{0,1},{1,2},{2,3},{3,4},{4,5},{5,6},{6,7},{8,9},{9,10},{10,11},{11... | collective-permute-start | bytes 93032 | tf_op jit(solution)/shard_map/ppermute | solution.py:20
  45.6 0.8 %copy-start.6 = (f32[3,4,8,128]{3,2,1,0:T(8,128)S(1)}, f32[3,4,8,128]{3,2,1,0:T(8,128)}, u32[]{:S(2)}) copy-start(f32[3,4,8,128]{3,2,1,0:T(8,128)} %param.26) | copy-start | bytes 147460
  47.7 0.7 copy-start.12
  48.5 5.5 %copy-start.1 = (f32[3,3,4,8,128]{4,3,2,1,0:T(8,128)S(1)}, f32[3,3,4,8,128]{4,3,2,1,0:T(8,128)}, u32[]{:S(2)}) copy-start(f32[3,3,4,8,128]{4,3,2,1,0:T(8,128)} %param.27) | copy-start | bytes 442372
  48.6 6.6 %collective-permute-start.4 = (f32[3,1,4,646]{3,2,1,0:T(4,128)S(1)}, f32[3,1,4,646]{3,2,1,0:T(4,128)S(1)}, u32[]{:S(2)}, u32[]{:S(2)}) collective-permute-start(f32[3,1,4,646]{3,2,1,0:T(4,128)S(1)} %get-tuple-element.47), channel_id=1, source_target_pairs={{8,0},{16,8},{24,16},{32,24},{40,32},{48,40},{56,48},{64,56},{72,6... | collective-permute-start | bytes 93032 | tf_op jit(solution)/shard_map/ppermute | solution.py:22
  50.5 12.9 %collective-permute-start.5 = (f32[3,1,4,646]{3,2,1,0:T(4,128)S(1)}, f32[3,1,4,646]{3,2,1,0:T(4,128)S(1)}, u32[]{:S(2)}, u32[]{:S(2)}) collective-permute-start(f32[3,1,4,646]{3,2,1,0:T(4,128)S(1)} %get-tuple-element.46), channel_id=1, source_target_pairs={{0,8},{8,16},{16,24},{24,32},{32,40},{40,48},{48,56},{56,64},{64,7... | collective-permute-start | bytes 93032 | tf_op jit(solution)/shard_map/ppermute | solution.py:20
  63.7 7.4 %collective-permute-start.6 = (f32[3,4,1,646]{3,2,1,0:T(1,128)S(1)}, f32[3,4,1,646]{3,2,1,0:T(1,128)S(1)}, u32[]{:S(2)}, u32[]{:S(2)}) collective-permute-start(f32[3,4,1,646]{3,2,1,0:T(1,128)S(1)} %get-tuple-element.38), channel_id=1, source_target_pairs={{1,0},{2,1},{3,2},{4,3},{5,4},{6,5},{7,6},{9,8},{10,9},{11,10},{12... | collective-permute-start | bytes 93032 | tf_op jit(solution)/shard_map/ppermute | solution.py:22
  65.6 6.3 %collective-permute-start.7 = (f32[3,4,1,646]{3,2,1,0:T(1,128)S(1)}, f32[3,4,1,646]{3,2,1,0:T(1,128)S(1)}, u32[]{:S(2)}, u32[]{:S(2)}) collective-permute-start(f32[3,4,1,646]{3,2,1,0:T(1,128)S(1)} %get-tuple-element.39), channel_id=1, source_target_pairs={{0,1},{1,2},{2,3},{3,4},{4,5},{5,6},{6,7},{8,9},{9,10},{10,11},{11... | collective-permute-start | bytes 93032 | tf_op jit(solution)/shard_map/ppermute | solution.py:20
where the time goes:
time: 77.1 us; the launch traced here: 76.3 us
  starting transfers between devices  37.1 us (48%)
  waiting for transfers between devices  20.2 us (26%)
  local copies, waits for them, and re-layouts  9.29 us (12%)
  other arithmetic  8.43 us (11%)
  between operations  1.25 us (2%)
    ppermute x4, starting transfers between devices, padded_2(): lax.ppermute(head, axis, [((i + 1) % count, i) for i in range(ends)])  22.9 us
    ppermute x4, waiting for transfers between devices, padded_2(): lax.ppermute(tail, axis, [(i, (i + 1) % count) for i in range(ends)])  20.2 us
    ppermute x4, starting transfers between devices, padded_2(): lax.ppermute(tail, axis, [(i, (i + 1) % count) for i in range(ends)])  14.2 us
    unnamed x32, local copies, waits for them, and re-layouts  4.44 us
  transfers between devices with their start and end apart: 8, of which 4 were waited for; matrix products, arithmetic and copies ran while one was open for 2% of the time, Pallas kernels for 0%

commit v1 on v0

v1 whole, which is shorter than its diff:
```python
import jax
import jax.numpy as jnp
from jax import lax
from jax.experimental import pallas as pl
from jax.experimental.pallas import tpu as pltpu
from jax.sharding import PartitionSpec as P

DT = 0.1
F32 = jnp.float32
LANES = 128

YT = 44
XT = 35


def lane_roll(tile, by):
    return pltpu.roll(tile, by % LANES, axis=1)


def row_roll(tile, by):
    return pltpu.roll(tile, by % tile.shape[0], axis=0)


def relax(u, mem, q, om):
    nxt = [[mem[l][c] + DT * om[l] * (u[c] - mem[l][c]) for c in range(3)] for l in range(3)]
    old = [sum(q[l] * mem[l][c] for l in range(3)) for c in range(3)]
    new = [sum(q[l] * nxt[l][c] for l in range(3)) for c in range(3)]
    return old, nxt, new


def pre_kernel(uc, pc, mc, muc, lamc, rhoc, qc, omc, uf, pf, mf, muf, lamf, rhof, qf, omf, st, out1, out2, own_f, own_c):
    even = lax.rem(lax.axis_index("gy"), 2) == 0
    eye = lax.broadcasted_iota(jnp.int32, (8, 8), 0) == lax.broadcasted_iota(jnp.int32, (8, 8), 1)

    def level(u_r, p_r, m_r, mu_r, lam_r, rho_r, q_r, om_r, own, wide):
        for x in range(wide):
            u = [u_r[c, x] for c in range(3)]
            mem = [[m_r[l, c, x] for c in range(3)] for l in range(3)]
            old, _, new = relax(u, mem, [q_r[l, x] for l in range(3)], [om_r[l, x] for l in range(3)])
            scale = (DT * DT) / rho_r[x]
            mu = mu_r[x]
            for c in range(3):
                own[c * wide + x] = u[c] - old[c]
                own[(3 + c) * wide + x] = 2.0 * u[c] - p_r[c, x] - new[c]
            own[6 * wide + x] = scale * mu
            own[7 * wide + x] = scale * (lam_r[x] + mu)

    level(uf, pf, mf, muf, lamf, rhof, qf, omf, own_f, 4)
    level(uc, pc, mc, muc, lamc, rhoc, qc, omc, own_c, 2)
    for x in range(4):
        row = jnp.broadcast_to(st[x : x + 1, :], (8, 8))
        col = jnp.sum(jnp.where(eye, row, 0.0), axis=1, keepdims=True)
        own_f[32 + x] = 1.0 / jnp.broadcast_to(col, (8, LANES))

    def message(out, up):
        for k in range(36):
            out[k] = own_f[k, 4:8] if up else own_f[k, 0:4]
        for f in range(8):
            for x in range(2):
                out[36 + f, 2 * x : 2 * x + 2] = own_c[2 * f + x, 2:4] if up else own_c[2 * f + x, 0:2]

    @pl.when(even)
    def _():
        message(out1, True)
        message(out2, False)

    @pl.when(jnp.logical_not(even))
    def _():
        message(out1, False)
        message(out2, True)


def mid_kernel(own_f, own_c, r1, r2, ext_f, ext_c, out1, out2):
    even_y = lax.rem(lax.axis_index("gy"), 2) == 0
    even_x = lax.rem(lax.axis_index("gx"), 2) == 0
    for k in range(36):
        ext_f[k, 0:8] = own_f[k]
    for k in range(16):
        ext_c[k, 0:4] = own_c[k]

    def place(above, below):
        for k in range(36):
            ext_f[k, 8:12] = above[k]
            ext_f[k, 12:16] = below[k]
        for f in range(8):
            for x in range(2):
                ext_c[2 * f + x, 4:6] = above[36 + f, 2 * x : 2 * x + 2]
                ext_c[2 * f + x, 6:8] = below[36 + f, 2 * x : 2 * x + 2]

    @pl.when(even_y)
    def _():
        place(r1, r2)

    @pl.when(jnp.logical_not(even_y))
    def _():
        place(r2, r1)

    lane = lax.broadcasted_iota(jnp.int32, (16, LANES), 1)

    def message(out, right):
        def col(ring):
            return 4 - ring if right else ring - 1

        near = 1 if right else 0
        for c in range(3):
            for x in range(2):
                out[2 * c + x] = ext_c[2 * c + x]
            out[6 + c] = ext_c[2 * (3 + c) + near]
        out[9] = ext_c[12 + near]
        out[10] = ext_c[14 + near]

        def put(k, tile):
            out[11 + 2 * k] = tile[0:8]
            out[12 + 2 * k] = tile[8:16]

        for c in range(3):
            put(c, ext_f[4 * c + col(1)])
            put(3 + c, ext_f[4 * c + col(2)])
            put(6 + c, ext_f[4 * (3 + c) + col(1)])
        put(9, ext_f[24 + col(1)])
        put(10, ext_f[28 + col(1)])
        bits = jnp.where(lane == 17, ext_f[32 + col(1)], ext_f[32 + col(2)])
        for c in range(3):
            for r in range(2):
                at = 4 * c + 2 * r
                both = jnp.logical_or(lane == at, lane == at + 1)
                bits = jnp.where(both, lane_roll(ext_f[4 * c + col(3 + r)], at + 2), bits)
            bits = jnp.where(lane == 12 + c, lane_roll(ext_f[4 * (3 + c) + col(2)], 13 + c), bits)
        bits = jnp.where(lane == 15, lane_roll(ext_f[24 + col(2)], 16), bits)
        bits = jnp.where(lane == 16, lane_roll(ext_f[28 + col(2)], 17), bits)
        put(11, bits)

    @pl.when(even_x)
    def _():
        message(out1, True)
        message(out2, False)

    @pl.when(jnp.logical_not(even_x))
    def _():
        message(out1, False)
        message(out2, True)


def operator(w, zp, zm, x, inv_h2, inv_flat, inv_slant, inv_hz2):
    def dz(c, at):
        return zp[c, at] - zm[c, at]

    def up(tile):
        return row_roll(tile, -1)

    def down(tile):
        return row_roll(tile, 1)

    def dy(c, at):
        return up(w[c, at]) - down(w[c, at])

    dxx = [w[c, x + 1] + w[c, x - 1] - 2.0 * w[c, x] for c in range(3)]
    dyy = [up(w[c, x]) + down(w[c, x]) - 2.0 * w[c, x] for c in range(3)]
    dzz = [zp[c, x] + zm[c, x] - 2.0 * w[c, x] for c in range(3)]
    lap = [(dxx[c] + dyy[c]) * inv_h2 + dzz[c] * inv_hz2 for c in range(3)]
    yz = [up(dz(c, x)) - down(dz(c, x)) for c in (1, 2)]
    grad = [
        dxx[0] * inv_h2 + (dy(1, x + 1) - dy(1, x - 1)) * inv_flat + (dz(2, x + 1) - dz(2, x - 1)) * inv_slant,
        (dy(0, x + 1) - dy(0, x - 1)) * inv_flat + dyy[1] * inv_h2 + yz[1] * inv_slant,
        (dz(0, x + 1) - dz(0, x - 1) + yz[0]) * inv_slant + dzz[2] * inv_hz2,
    ]
    return lap, grad


def post_kernel(ext_f, ext_c, r1, r2, uc, mc, qc, omc, uf, mf, qf, omf, uc_out, uf_out, mc_out, mf_out, halo, scr):
    gx, gy = lax.axis_index("gx"), lax.axis_index("gy")
    even_x = lax.rem(gx, 2) == 0

    @pl.when(even_x)
    def _():
        halo[0] = r2[...]
        halo[1] = r1[...]

    @pl.when(jnp.logical_not(even_x))
    def _():
        halo[0] = r1[...]
        halo[1] = r2[...]

    slots = [0]

    def slot():
        slots[0] += 1
        return slots[0] - 1

    lane_f = lax.broadcasted_iota(jnp.int32, (16, LANES), 1)
    lane_c = lax.broadcasted_iota(jnp.int32, (8, LANES), 1)
    row = lax.broadcasted_iota(jnp.int32, (16, LANES), 0)
    outside_y = jnp.logical_or(
        jnp.logical_and(row >= 12, gy == 0),
        jnp.logical_and(jnp.logical_and(row >= 8, row < 12), gy == lax.axis_size("gy") - 1),
    )
    keep_y = jnp.where(outside_y, 0.0, 1.0).astype(F32)
    keep_left = jnp.where(gx == 0, 0.0, 1.0).astype(F32)
    keep_right = jnp.where(gx == lax.axis_size("gx") - 1, 0.0, 1.0).astype(F32)

    def pair(side, k):
        return jnp.concatenate([halo[side, 11 + 2 * k], halo[side, 12 + 2 * k]], axis=0)

    wf, wc, af, ac, cf, cc, rz = {}, {}, {}, {}, {}, {}, {}
    for c in range(3):
        for x in range(4):
            wf[c, x] = ext_f[4 * c + x]
            af[c, x] = ext_f[4 * (3 + c) + x]
        for x in range(2):
            wc[c, x] = ext_c[2 * c + x]
            ac[c, x] = ext_c[2 * (3 + c) + x]
    for t in range(2):
        for x in range(4):
            cf[t, x] = ext_f[4 * (6 + t) + x]
        for x in range(2):
            cc[t, x] = ext_c[2 * (6 + t) + x]
    for x in range(4):
        rz[x] = ext_f[32 + x]
    for side in range(2):

        def col(ring):
            return 3 + ring if side else -ring

        bits = pair(side, 11)
        near = 2 if side else -1
        for c in range(3):
            for x in range(2):
                wc[c, (2 if side else -2) + x] = halo[side, 2 * c + x]
            ac[c, near] = halo[side, 6 + c]
            wf[c, col(1)] = pair(side, c)
            wf[c, col(2)] = pair(side, 3 + c)
            for r in range(2):
                wf[c, col(3 + r)] = lane_roll(bits, 126 - 4 * c - 2 * r)
            af[c, col(1)] = pair(side, 6 + c)
            af[c, col(2)] = lane_roll(bits, 115 - c)
        for t in range(2):
            cc[t, near] = halo[side, 9 + t]
            cf[t, col(1)] = pair(side, 9 + t)
            cf[t, col(2)] = lane_roll(bits, 112 - t)
            rz[col(1 + t)] = jnp.broadcast_to(bits[:, 17 + t : 18 + t], (16, LANES))

    def prolong(field, c, x):
        cx = x // 2
        tile = 0.75 * field[c, cx] + 0.25 * field[c, cx + 1 if x % 2 else cx - 1]
        at = slot()
        scr[at, pl.ds(0, 8, stride=2), :] = 0.75 * tile + 0.25 * row_roll(tile, 1)
        scr[at, pl.ds(1, 8, stride=2), :] = 0.75 * tile + 0.25 * row_roll(tile, -1)
        out = scr[at] * keep_y
        return out * keep_left if x < 0 else out * keep_right if x > 3 else out

    def restrict(field, c, cx):
        at = slot()
        scr[at] = field[c, 2 * cx] + field[c, 2 * cx + 1]
        return 0.25 * (scr[at, pl.ds(0, 8, stride=2), :] + scr[at, pl.ds(1, 8, stride=2), :])

    def neighbours(fine, coarse, reach_f, reach_c):
        zp_f, zm_f, zp_c, zm_c = {}, {}, {}, {}
        for c in range(3):
            for x in reach_f:
                tile = fine[c, x]
                zp_f[c, x] = jnp.where(lane_f == LANES - 1, lane_roll(prolong(coarse, c, x), -1), lane_roll(tile, -1))
                zm_f[c, x] = jnp.where(lane_f == 0, tile, lane_roll(tile, 1))
            for x in reach_c:
                tile = coarse[c, x]
                zp_c[c, x] = jnp.where(lane_c == LANES - 1, 0.0, lane_roll(tile, -1))
                zm_c[c, x] = jnp.where(lane_c == 0, lane_roll(restrict(fine, c, x), 1), lane_roll(tile, 1))
        return zp_f, zm_f, zp_c, zm_c

    zp_f, zm_f, zp_c, zm_c = neighbours(wf, wc, range(-3, 7), range(-2, 4))
    wf1, wc1 = {}, {}
    for x in range(-2, 6):
        lap, grad = operator(wf, zp_f, zm_f, x, 4.0, 1.0, 0.5 * rz[x], rz[x] * rz[x])
        for c in range(3):
            wf1[c, x] = af[c, x] + cf[0, x] * lap[c] + cf[1, x] * grad[c]
    for x in range(-1, 3):
        lap, grad = operator(wc, zp_c, zm_c, x, 1.0, 0.25, 0.25, 1.0)
        for c in range(3):
            wc1[c, x] = ac[c, x] + cc[0, x] * lap[c] + cc[1, x] * grad[c]

    zp_f, zm_f, zp_c, zm_c = neighbours(wf1, wc1, range(-1, 5), range(-1, 3))

    def finish(w1, lap, grad, c0, c1, u_r, m_r, q_r, om_r, u_out, m_out, x, tall):
        u = [u_r[c, x] for c in range(3)]
        om = [om_r[l, x] for l in range(3)]
        mem = [[m_r[l, c, x] for c in range(3)] for l in range(3)]
        _, nxt, new = relax(u, mem, [q_r[l, x] for l in range(3)], om)
        for c in range(3):
            u1 = w1[c, x][0:tall] + new[c]
            u_out[c, x] = 2.0 * u1 - u[c] + (c0 * lap[c] + c1 * grad[c])[0:tall]
            for l in range(3):
                m_out[l, c, x] = nxt[l][c] + DT * om[l] * (u1 - nxt[l][c])

    for x in range(4):
        lap, grad = operator(wf1, zp_f, zm_f, x, 4.0, 1.0, 0.5 * rz[x], rz[x] * rz[x])
        finish(wf1, lap, grad, cf[0, x], cf[1, x], uf, mf, qf, omf, uf_out, mf_out, x, 8)
    for x in range(2):
        lap, grad = operator(wc1, zp_c, zm_c, x, 1.0, 0.25, 0.25, 1.0)
        finish(wc1, lap, grad, cc[0, x], cc[1, x], uc, mc, qc, omc, uc_out, mc_out, x, 4)


SCRATCH = 3 * (10 + 6 + 6 + 4)


def swap(value, axis, first):
    pairs = []
    for i in range(first, lax.axis_size(axis) - 1, 2):
        pairs += [(i, i + 1), (i + 1, i)]
    return lax.ppermute(value, axis, pairs)


def call(kernel, shapes, scratch=()):
    vmem = pl.BlockSpec(memory_space=pltpu.VMEM)

    def run(*args):
        return pl.pallas_call(
            kernel,
            out_shape=[jax.ShapeDtypeStruct(s, F32) for s in shapes],
            in_specs=[vmem] * len(args),
            out_specs=[vmem] * len(shapes),
            scratch_shapes=list(scratch),
        )(*args)

    return run


def shards(
    u_now_c,
    u_prev_c,
    memory_c,
    mu_c,
    lam_c,
    rho_c,
    q_c,
    omega_c,
    u_now_f,
    u_prev_f,
    memory_f,
    mu_f,
    lam_f,
    rho_f,
    q_f,
    omega_f,
    stretch_f,
):
    up, down, own_f, own_c = call(pre_kernel, [(YT, 4, LANES)] * 2 + [(36, 8, LANES), (16, 4, LANES)])(
        u_now_c, u_prev_c, memory_c, mu_c, lam_c, rho_c, q_c, omega_c,
        u_now_f, u_prev_f, memory_f, mu_f, lam_f, rho_f, q_f, omega_f, stretch_f,
    )
    r2 = swap(down, "gy", 1)
    r1 = swap(up, "gy", 0)
    ext_f, ext_c, right, left = call(mid_kernel, [(36, 16, LANES), (16, 8, LANES)] + [(XT, 8, LANES)] * 2)(
        own_f, own_c, r1, r2
    )
    s2 = swap(left, "gx", 1)
    s1 = swap(right, "gx", 0)
    return tuple(
        call(
            post_kernel,
            [u_now_c.shape, u_now_f.shape, memory_c.shape, memory_f.shape],
            [pltpu.VMEM((2, XT, 8, LANES), F32), pltpu.VMEM((SCRATCH, 16, LANES), F32)],
        )(ext_f, ext_c, s1, s2, u_now_c, memory_c, q_c, omega_c, u_now_f, memory_f, q_f, omega_f)
    )


def solution(mesh):
    def level(*lead):
        return P(*lead, "gx", "gy", None)

    inputs = (level(None), level(None), level(None, None), level(), level(), level(), level(None), level(None))
    return jax.shard_map(
        shards,
        mesh=mesh,
        in_specs=inputs + inputs + (P("gx", "gy"),),
        out_specs=(level(None), level(None), level(None, None), level(None, None)),
        check_vma=False,
    )
```

time: 77.1 us -> 47.8 us (0.62)
  the two profiles are of different devices: /device:TPU:33 before, /device:TPU:57 now
where the time goes in v1:
time: 47.8 us; the launch traced here: 47.6 us
  starting transfers between devices  25.9 us (54%)
  waiting for transfers between devices  13.2 us (28%)
  Pallas kernels  6.51 us (14%)
  local copies, waits for them, and re-layouts  1.29 us (3%)
  between operations  0.7 us (1%)
    ppermute x4, starting transfers between devices, swap(): return lax.ppermute(value, axis, pairs)  25.9 us
    ppermute x4, waiting for transfers between devices, swap(): return lax.ppermute(value, axis, pairs)  13.2 us
    pallas_call x3, Pallas kernels, run(): pl.pallas_call(kernel, out_shape=[jax.ShapeDtypeStruct(s, F32) for s in s...  6.51 us
    unnamed x8, local copies, waits for them, and re-layouts  1.29 us
  transfers between devices with their start and end apart: 4, of which 2 were waited for; matrix products, arithmetic and copies ran while one was open for 0% of the time, Pallas kernels for 0%

profile of v1, /device:TPU:57, one launch (start us, length us, event | category | flops | bytes accessed | tf_op | source)
XLA Modules:
  0.0 47.6 jit_solution(11688111564432892845)
XLA Ops:
  0.6 2.0 %shard_map.192 = (f32[44,4,128]{2,1,0:T(4,128)}, f32[44,4,128]{2,1,0:T(4,128)}, f32[36,8,128]{2,1,0:T(8,128)}, f32[16,4,128]{2,1,0:T(4,128)}) custom-call(f32[3,2,4,128]{3,2,1,0:T(4,128)} %uc.3, f32[3,2,4,128]{3,2,1,0:T(4,128)} %pc.1, f32[3,3,2,4,128]{4,3,2,1,0:T(4,128)} %mc.3, f32[2,4,128]{2,1,0:T(4,128)} %muc.1, f32[2,4,128]{2,1,0:T(4,128)} %lamc.1, ...), custom_call_target="tpu_custom_call" | custom-call | tf_op jit(solution)/shard_map/pallas_call | solution.py:315
  2.6 2.6 %collective-permute-start = (f32[44,4,128]{2,1,0:T(4,128)}, f32[44,4,128]{2,1,0:T(4,128)S(1)}, u32[]{:S(2)}, u32[]{:S(2)}) collective-permute-start(f32[44,4,128]{2,1,0:T(4,128)} %get-tuple-element.14), channel_id=1, source_target_pairs={{0,1},{1,0},{2,3},{3,2},{4,5},{5,4},{6,7},{7,6},{8,9},{9,8},{10,11... | collective-permute-start | bytes 270344 | tf_op jit(solution)/shard_map/ppermute | solution.py:308
  5.2 3.9 %collective-permute-start.1 = (f32[44,4,128]{2,1,0:T(4,128)}, f32[44,4,128]{2,1,0:T(4,128)S(1)}, u32[]{:S(2)}, u32[]{:S(2)}) collective-permute-start(f32[44,4,128]{2,1,0:T(4,128)} %get-tuple-element.15), channel_id=1, source_target_pairs={{1,2},{2,1},{3,4},{4,3},{5,6},{6,5},{9,10},{10,9},{11,12},{12,11},... | collective-permute-start | bytes 270344 | tf_op jit(solution)/shard_map/ppermute | solution.py:308
  9.1 0.0 collective-permute-done.r1
  9.1 0.0 copy-start.2
  9.1 2.4 %collective-permute-done.1.r2 = f32[44,4,128]{2,1,0:T(4,128)S(1)} collective-permute-done((f32[44,4,128]{2,1,0:T(4,128)}, f32[44,4,128]{2,1,0:T(4,128)S(1)}, u32[]{:S(2)}, u32[]{:S(2)}) %collective-permute-start.1) | collective-permute-done | bytes 90144 | tf_op jit(solution)/shard_map/ppermute | solution.py:308
  11.5 0.0 copy-start.3
  11.5 0.0 copy-done.2
  11.5 0.6 %copy-done.3 = f32[44,4,128]{2,1,0:T(4,128)} copy-done((f32[44,4,128]{2,1,0:T(4,128)}, f32[44,4,128]{2,1,0:T(4,128)S(1)}, u32[]{:S(2)}) %copy-start.3) | copy-done | bytes 90136
  12.1 2.0 %shard_map.193 = (f32[36,16,128]{2,1,0:T(8,128)}, f32[16,8,128]{2,1,0:T(8,128)}, f32[35,8,128]{2,1,0:T(8,128)}, f32[35,8,128]{2,1,0:T(8,128)}) custom-call(f32[36,8,128]{2,1,0:T(8,128)} %get-tuple-element.12.own_f, f32[16,4,128]{2,1,0:T(4,128)} %get-tuple-element.13.own_c, f32[44,4,128]{2,1,0:T(4,128)} %copy-done.2, f32[44,4,128]{2,1,0:T(4,128)} %copy-done.3), custom_call_target="tpu_custom_call" | custom-call | tf_op jit(solution)/shard_map/pallas_call | solution.py:315
  14.2 3.1 %collective-permute-start.2 = (f32[35,8,128]{2,1,0:T(8,128)}, f32[35,8,128]{2,1,0:T(8,128)S(1)}, u32[]{:S(2)}, u32[]{:S(2)}) collective-permute-start(f32[35,8,128]{2,1,0:T(8,128)} %get-tuple-element.18), channel_id=1, source_target_pairs={{0,8},{8,0},{16,24},{24,16},{32,40},{40,32},{48,56},{56,48},{64,72... | collective-permute-start | bytes 430088 | tf_op jit(solution)/shard_map/ppermute | solution.py:308
  17.3 16.3 %collective-permute-start.3 = (f32[35,8,128]{2,1,0:T(8,128)}, f32[35,8,128]{2,1,0:T(8,128)S(1)}, u32[]{:S(2)}, u32[]{:S(2)}) collective-permute-start(f32[35,8,128]{2,1,0:T(8,128)} %get-tuple-element.19), channel_id=1, source_target_pairs={{8,16},{16,8},{24,32},{32,24},{40,48},{48,40},{56,64},{64,56},{72,... | collective-permute-start | bytes 430088 | tf_op jit(solution)/shard_map/ppermute | solution.py:308
  33.6 0.0 collective-permute-done.2.r1
  33.6 0.0 copy-start
  33.6 10.8 %collective-permute-done.3.r2 = f32[35,8,128]{2,1,0:T(8,128)S(1)} collective-permute-done((f32[35,8,128]{2,1,0:T(8,128)}, f32[35,8,128]{2,1,0:T(8,128)S(1)}, u32[]{:S(2)}, u32[]{:S(2)}) %collective-permute-start.3) | collective-permute-done | bytes 143392 | tf_op jit(solution)/shard_map/ppermute | solution.py:308
  44.4 0.0 copy-start.1
  44.4 0.0 copy-done
  44.4 0.6 %copy-done.1 = f32[35,8,128]{2,1,0:T(8,128)} copy-done((f32[35,8,128]{2,1,0:T(8,128)}, f32[35,8,128]{2,1,0:T(8,128)S(1)}, u32[]{:S(2)}) %copy-start.1) | copy-done | bytes 143384
  45.1 2.5 %shard_map.194 = (f32[3,2,4,128]{3,2,1,0:T(4,128)}, f32[3,4,8,128]{3,2,1,0:T(8,128)}, f32[3,3,2,4,128]{4,3,2,1,0:T(4,128)}, f32[3,3,4,8,128]{4,3,2,1,0:T(8,128)}) custom-call(f32[36,16,128]{2,1,0:T(8,128)} %get-tuple-element.16.ext_f, f32[16,8,128]{2,1,0:T(8,128)} %get-tuple-element.17.ext_c, f32[35,8,128]{2,1,0:T(8,128)} %copy-done, ...), custom_call_target="tpu_custom_call" | custom-call | tf_op jit(solution)/shard_map/pallas_call | solution.py:315
Async XLA Ops:
  2.6 6.5 %collective-permute-start = (f32[44,4,128]{2,1,0:T(4,128)}, f32[44,4,128]{2,1,0:T(4,128)S(1)}, u32[]{:S(2)}, u32[]{:S(2)}) collective-permute-start(f32[44,4,128]{2,1,0:T(4,128)} %get-tuple-element.14), channel_id=1, source_target_pairs={{0,1},{1,0},{2,3},{3,2},{4,5},{5,4},{6,7},{7,6},{8,9},{9,8},{10,11... | collective-permute-start | bytes 270344 | tf_op jit(solution)/shard_map/ppermute | solution.py:308
  5.2 6.3 %collective-permute-start.1 = (f32[44,4,128]{2,1,0:T(4,128)}, f32[44,4,128]{2,1,0:T(4,128)S(1)}, u32[]{:S(2)}, u32[]{:S(2)}) collective-permute-start(f32[44,4,128]{2,1,0:T(4,128)} %get-tuple-element.15), channel_id=1, source_target_pairs={{1,2},{2,1},{3,4},{4,3},{5,6},{6,5},{9,10},{10,9},{11,12},{12,11},... | collective-permute-start | bytes 270344 | tf_op jit(solution)/shard_map/ppermute | solution.py:308
  9.1 2.4 %copy-start.2 = (f32[44,4,128]{2,1,0:T(4,128)}, f32[44,4,128]{2,1,0:T(4,128)S(1)}, u32[]{:S(2)}) copy-start(f32[44,4,128]{2,1,0:T(4,128)S(1)} %collective-permute-done.r1) | copy-start | bytes 270340
  11.5 0.6 %copy-start.3 = (f32[44,4,128]{2,1,0:T(4,128)}, f32[44,4,128]{2,1,0:T(4,128)S(1)}, u32[]{:S(2)}) copy-start(f32[44,4,128]{2,1,0:T(4,128)S(1)} %collective-permute-done.1.r2) | copy-start | bytes 270340
  14.2 19.5 %collective-permute-start.2 = (f32[35,8,128]{2,1,0:T(8,128)}, f32[35,8,128]{2,1,0:T(8,128)S(1)}, u32[]{:S(2)}, u32[]{:S(2)}) collective-permute-start(f32[35,8,128]{2,1,0:T(8,128)} %get-tuple-element.18), channel_id=1, source_target_pairs={{0,8},{8,0},{16,24},{24,16},{32,40},{40,32},{48,56},{56,48},{64,72... | collective-permute-start | bytes 430088 | tf_op jit(solution)/shard_map/ppermute | solution.py:308
  17.3 27.1 %collective-permute-start.3 = (f32[35,8,128]{2,1,0:T(8,128)}, f32[35,8,128]{2,1,0:T(8,128)S(1)}, u32[]{:S(2)}, u32[]{:S(2)}) collective-permute-start(f32[35,8,128]{2,1,0:T(8,128)} %get-tuple-element.19), channel_id=1, source_target_pairs={{8,16},{16,8},{24,32},{32,24},{40,48},{48,40},{56,64},{64,56},{72,... | collective-permute-start | bytes 430088 | tf_op jit(solution)/shard_map/ppermute | solution.py:308
  33.6 10.8 %copy-start = (f32[35,8,128]{2,1,0:T(8,128)}, f32[35,8,128]{2,1,0:T(8,128)S(1)}, u32[]{:S(2)}) copy-start(f32[35,8,128]{2,1,0:T(8,128)S(1)} %collective-permute-done.2.r1) | copy-start | bytes 430084
  44.4 0.7 %copy-start.1 = (f32[35,8,128]{2,1,0:T(8,128)}, f32[35,8,128]{2,1,0:T(8,128)S(1)}, u32[]{:S(2)}) copy-start(f32[35,8,128]{2,1,0:T(8,128)S(1)} %collective-permute-done.3.r2) | copy-start | bytes 430084

commit v2 on v1

--- a/solution.py
+++ b/solution.py
@@ -70,7 +70,7 @@
         message(out2, True)
 
 
-def mid_kernel(own_f, own_c, r1, r2, ext_f, ext_c, out1, out2):
+def mid_kernel(own_f, own_c, r2, r1, ext_f, ext_c, out1, out2):
     even_y = lax.rem(lax.axis_index("gy"), 2) == 0
     even_x = lax.rem(lax.axis_index("gx"), 2) == 0
     for k in range(36):
@@ -167,7 +167,7 @@
     return lap, grad
 
 
-def post_kernel(ext_f, ext_c, r1, r2, uc, mc, qc, omc, uf, mf, qf, omf, uc_out, uf_out, mc_out, mf_out, halo, scr):
+def post_kernel(ext_f, ext_c, r2, r1, uc, mc, qc, omc, uf, mf, qf, omf, uc_out, uf_out, mc_out, mf_out, halo, scr):
     gx, gy = lax.axis_index("gx"), lax.axis_index("gy")
     even_x = lax.rem(gx, 2) == 0
 
@@ -308,13 +308,15 @@
     return lax.ppermute(value, axis, pairs)
 
 
-def call(kernel, shapes, scratch=()):
+def call(kernel, shapes, scratch=(), first=False, last=False):
     vmem = pl.BlockSpec(memory_space=pltpu.VMEM)
 
     def run(*args):
+        if not first:
+            args = [pltpu.with_memory_space_constraint(a, pltpu.VMEM) for a in args]
         return pl.pallas_call(
             kernel,
-            out_shape=[jax.ShapeDtypeStruct(s, F32) for s in shapes],
+            out_shape=[(jax.ShapeDtypeStruct if last else pltpu.VMEM)(s, F32) for s in shapes],
             in_specs=[vmem] * len(args),
             out_specs=[vmem] * len(shapes),
             scratch_shapes=list(scratch),
@@ -342,14 +344,14 @@
     omega_f,
     stretch_f,
 ):
-    up, down, own_f, own_c = call(pre_kernel, [(YT, 4, LANES)] * 2 + [(36, 8, LANES), (16, 4, LANES)])(
+    up, down, own_f, own_c = call(pre_kernel, [(YT, 4, LANES)] * 2 + [(36, 8, LANES), (16, 4, LANES)], first=True)(
         u_now_c, u_prev_c, memory_c, mu_c, lam_c, rho_c, q_c, omega_c,
         u_now_f, u_prev_f, memory_f, mu_f, lam_f, rho_f, q_f, omega_f, stretch_f,
     )
     r2 = swap(down, "gy", 1)
     r1 = swap(up, "gy", 0)
     ext_f, ext_c, right, left = call(mid_kernel, [(36, 16, LANES), (16, 8, LANES)] + [(XT, 8, LANES)] * 2)(
-        own_f, own_c, r1, r2
+        own_f, own_c, r2, r1
     )
     s2 = swap(left, "gx", 1)
     s1 = swap(right, "gx", 0)
@@ -358,7 +360,8 @@
             post_kernel,
             [u_now_c.shape, u_now_f.shape, memory_c.shape, memory_f.shape],
             [pltpu.VMEM((2, XT, 8, LANES), F32), pltpu.VMEM((SCRATCH, 16, LANES), F32)],
-        )(ext_f, ext_c, s1, s2, u_now_c, memory_c, q_c, omega_c, u_now_f, memory_f, q_f, omega_f)
+            last=True,
+        )(ext_f, ext_c, s2, s1, u_now_c, memory_c, q_c, omega_c, u_now_f, memory_f, q_f, omega_f)
     )
 
 

time: 47.8 us -> 40.3 us (0.84)
  Pallas kernels: 6.51 us -> 2.73 us
  waiting for transfers between devices: 13.2 us -> 11.4 us
  local copies, waits for them, and re-layouts: 1.29 us -> 0.04 us
  starting transfers between devices: 25.9 us -> 24.7 us
    pallas_call x3, Pallas kernels: 6.51 us -> 2.73 us  [run(): pl.pallas_call(kernel, out_shape=[(jax.ShapeDtypeStruct if last else pltp...]
    ppermute x4, waiting for transfers between devices: 13.2 us -> 11.4 us  [swap(): return lax.ppermute(value, axis, pairs)]
    unnamed x8 -> x16, local copies, waits for them, and re-layouts: 1.29 us -> 0.04 us
    ppermute x4, starting transfers between devices: 25.9 us -> 24.7 us  [swap(): return lax.ppermute(value, axis, pairs)]
  transfers between devices with their start and end apart: 4 -> 4, of which waited for: 2 -> 3; matrix products, arithmetic and copies ran while one was open for 0% -> 0% of each run, Pallas kernels for 0% -> 0%
where the time goes in v2:
time: 40.3 us; the launch traced here: 39.6 us
  starting transfers between devices  24.7 us (61%)
  waiting for transfers between devices  11.4 us (28%)
  Pallas kernels  2.73 us (7%)
  between operations  0.76 us (2%)
    ppermute x4, starting transfers between devices, swap(): return lax.ppermute(value, axis, pairs)  24.7 us
    ppermute x4, waiting for transfers between devices, swap(): return lax.ppermute(value, axis, pairs)  11.4 us
    pallas_call x3, Pallas kernels, run(): pl.pallas_call(kernel, out_shape=[(jax.ShapeDtypeStruct if last else pltp...  2.73 us
  transfers between devices with their start and end apart: 4, of which 3 were waited for; matrix products, arithmetic and copies ran while one was open for 0% of the time, Pallas kernels for 0%

profile of v2, /device:TPU:57, one launch (start us, length us, event | category | flops | bytes accessed | tf_op | source)
XLA Modules:
  0.0 39.6 jit_solution(319610623626594763)
XLA Ops:
  0.6 1.3 %shard_map.192 = (f32[44,4,128]{2,1,0:T(4,128)S(1)}, f32[44,4,128]{2,1,0:T(4,128)S(1)}, f32[36,8,128]{2,1,0:T(8,128)S(1)}, f32[16,4,128]{2,1,0:T(4,128)S(1)}) custom-call(f32[3,2,4,128]{3,2,1,0:T(4,128)} %uc.3, f32[3,2,4,128]{3,2,1,0:T(4,128)} %pc.1, f32[3,3,2,4,128]{4,3,2,1,0:T(4,128)} %mc.3, f32[2,4,128]{2,1,0:T(4,128)} %muc.1, f32[2,4,128]{2,1,0:T(4,128)} %lamc.1, ...), custom_call_target="tpu_custom_call" | custom-call | tf_op jit(solution)/shard_map/pallas_call | solution.py:317
  1.9 4.5 %collective-permute-start = (f32[44,4,128]{2,1,0:T(4,128)S(1)}, f32[44,4,128]{2,1,0:T(4,128)S(1)}, u32[]{:S(2)}, u32[]{:S(2)}) collective-permute-start(f32[44,4,128]{2,1,0:T(4,128)S(1)} %get-tuple-element.14), channel_id=1, source_target_pairs={{1,2},{2,1},{3,4},{4,3},{5,6},{6,5},{9,10},{10,9},{11,12},{12,11},... | collective-permute-start | bytes 270344 | tf_op jit(solution)/shard_map/ppermute | solution.py:308
  6.5 1.9 %collective-permute-start.1 = (f32[44,4,128]{2,1,0:T(4,128)S(1)}, f32[44,4,128]{2,1,0:T(4,128)S(1)}, u32[]{:S(2)}, u32[]{:S(2)}) collective-permute-start(f32[44,4,128]{2,1,0:T(4,128)S(1)} %get-tuple-element.15), channel_id=1, source_target_pairs={{0,1},{1,0},{2,3},{3,2},{4,5},{5,4},{6,7},{7,6},{8,9},{9,8},{10,11... | collective-permute-start | bytes 270344 | tf_op jit(solution)/shard_map/ppermute | solution.py:308
  8.4 0.3 collective-permute-done.r2
  8.7 1.0 %collective-permute-done.1.r1 = f32[44,4,128]{2,1,0:T(4,128)S(1)} collective-permute-done((f32[44,4,128]{2,1,0:T(4,128)S(1)}, f32[44,4,128]{2,1,0:T(4,128)S(1)}, u32[]{:S(2)}, u32[]{:S(2)}) %collective-permute-start.1) | collective-permute-done | bytes 90144 | tf_op jit(solution)/shard_map/ppermute | solution.py:308
  9.6 0.0 copy-start.7
  9.6 0.0 copy-start
  9.6 0.0 copy-start.1
  9.6 0.0 copy-start.2
  9.7 0.0 copy-start.3
  9.7 0.0 copy-start.4
  9.7 0.0 copy-start.5
  9.7 0.0 copy-start.6
  9.7 0.2 shard_map.193
  9.9 16.4 %collective-permute-start.2 = (f32[35,8,128]{2,1,0:T(8,128)S(1)}, f32[35,8,128]{2,1,0:T(8,128)S(1)}, u32[]{:S(2)}, u32[]{:S(2)}) collective-permute-start(f32[35,8,128]{2,1,0:T(8,128)S(1)} %get-tuple-element.18), channel_id=1, source_target_pairs={{8,16},{16,8},{24,32},{32,24},{40,48},{48,40},{56,64},{64,56},{72,... | collective-permute-start | bytes 430088 | tf_op jit(solution)/shard_map/ppermute | solution.py:308
  26.2 1.9 %collective-permute-start.3 = (f32[35,8,128]{2,1,0:T(8,128)S(1)}, f32[35,8,128]{2,1,0:T(8,128)S(1)}, u32[]{:S(2)}, u32[]{:S(2)}) collective-permute-start(f32[35,8,128]{2,1,0:T(8,128)S(1)} %get-tuple-element.19), channel_id=1, source_target_pairs={{0,8},{8,0},{16,24},{24,16},{32,40},{40,32},{48,56},{56,48},{64,72... | collective-permute-start | bytes 430088 | tf_op jit(solution)/shard_map/ppermute | solution.py:308
  28.2 10.1 %collective-permute-done.2.r2 = f32[35,8,128]{2,1,0:T(8,128)S(1)} collective-permute-done((f32[35,8,128]{2,1,0:T(8,128)S(1)}, f32[35,8,128]{2,1,0:T(8,128)S(1)}, u32[]{:S(2)}, u32[]{:S(2)}) %collective-permute-start.2) | collective-permute-done | bytes 143392 | tf_op jit(solution)/shard_map/ppermute | solution.py:308
  38.3 0.0 collective-permute-done.3.r1
  38.3 0.0 copy-done.7
  38.3 0.0 copy-done
  38.3 0.0 copy-done.1
  38.3 0.0 copy-done.2
  38.3 0.0 copy-done.3
  38.3 0.0 copy-done.4
  38.3 0.0 copy-done.5
  38.3 0.0 copy-done.6
  38.3 1.3 %shard_map.194 = (f32[3,2,4,128]{3,2,1,0:T(4,128)}, f32[3,4,8,128]{3,2,1,0:T(8,128)}, f32[3,3,2,4,128]{4,3,2,1,0:T(4,128)}, f32[3,3,4,8,128]{4,3,2,1,0:T(8,128)}) custom-call(f32[36,16,128]{2,1,0:T(8,128)S(1)} %get-tuple-element.16.ext_f, f32[16,8,128]{2,1,0:T(8,128)S(1)} %get-tuple-element.17.ext_c, f32[35,8,128]{2,1,0:T(8,128)S(1)} %collective-permute-done.2.r2, ...), custom_call_target="tpu_custom_call" | custom-call | tf_op jit(solution)/shard_map/pallas_call | solution.py:317
Async XLA Ops:
  1.9 6.8 %collective-permute-start = (f32[44,4,128]{2,1,0:T(4,128)S(1)}, f32[44,4,128]{2,1,0:T(4,128)S(1)}, u32[]{:S(2)}, u32[]{:S(2)}) collective-permute-start(f32[44,4,128]{2,1,0:T(4,128)S(1)} %get-tuple-element.14), channel_id=1, source_target_pairs={{1,2},{2,1},{3,4},{4,3},{5,6},{6,5},{9,10},{10,9},{11,12},{12,11},... | collective-permute-start | bytes 270344 | tf_op jit(solution)/shard_map/ppermute | solution.py:308
  6.5 3.2 %collective-permute-start.1 = (f32[44,4,128]{2,1,0:T(4,128)S(1)}, f32[44,4,128]{2,1,0:T(4,128)S(1)}, u32[]{:S(2)}, u32[]{:S(2)}) collective-permute-start(f32[44,4,128]{2,1,0:T(4,128)S(1)} %get-tuple-element.15), channel_id=1, source_target_pairs={{0,1},{1,0},{2,3},{3,2},{4,5},{5,4},{6,7},{7,6},{8,9},{9,8},{10,11... | collective-permute-start | bytes 270344 | tf_op jit(solution)/shard_map/ppermute | solution.py:308
  9.6 28.6 %copy-start.7 = (f32[3,2,4,128]{3,2,1,0:T(4,128)S(1)}, f32[3,2,4,128]{3,2,1,0:T(4,128)}, u32[]{:S(2)}) copy-start(f32[3,2,4,128]{3,2,1,0:T(4,128)} %omc.3) | copy-start | bytes 36868
  9.6 28.6 %copy-start = (f32[3,3,4,8,128]{4,3,2,1,0:T(8,128)S(1)}, f32[3,3,4,8,128]{4,3,2,1,0:T(8,128)}, u32[]{:S(2)}) copy-start(f32[3,3,4,8,128]{4,3,2,1,0:T(8,128)} %mf.3) | copy-start | bytes 442372
  9.6 28.6 %copy-start.1 = (f32[3,4,8,128]{3,2,1,0:T(8,128)S(1)}, f32[3,4,8,128]{3,2,1,0:T(8,128)}, u32[]{:S(2)}) copy-start(f32[3,4,8,128]{3,2,1,0:T(8,128)} %uf.3) | copy-start | bytes 147460
  9.6 28.6 %copy-start.2 = (f32[3,4,8,128]{3,2,1,0:T(8,128)S(1)}, f32[3,4,8,128]{3,2,1,0:T(8,128)}, u32[]{:S(2)}) copy-start(f32[3,4,8,128]{3,2,1,0:T(8,128)} %qf.3) | copy-start | bytes 147460
  9.7 28.6 %copy-start.3 = (f32[3,4,8,128]{3,2,1,0:T(8,128)S(1)}, f32[3,4,8,128]{3,2,1,0:T(8,128)}, u32[]{:S(2)}) copy-start(f32[3,4,8,128]{3,2,1,0:T(8,128)} %omf.3) | copy-start | bytes 147460
  9.7 28.6 %copy-start.4 = (f32[3,3,2,4,128]{4,3,2,1,0:T(4,128)S(1)}, f32[3,3,2,4,128]{4,3,2,1,0:T(4,128)}, u32[]{:S(2)}) copy-start(f32[3,3,2,4,128]{4,3,2,1,0:T(4,128)} %mc.3) | copy-start | bytes 110596
  9.7 28.6 %copy-start.5 = (f32[3,2,4,128]{3,2,1,0:T(4,128)S(1)}, f32[3,2,4,128]{3,2,1,0:T(4,128)}, u32[]{:S(2)}) copy-start(f32[3,2,4,128]{3,2,1,0:T(4,128)} %uc.3) | copy-start | bytes 36868
  9.7 28.6 %copy-start.6 = (f32[3,2,4,128]{3,2,1,0:T(4,128)S(1)}, f32[3,2,4,128]{3,2,1,0:T(4,128)}, u32[]{:S(2)}) copy-start(f32[3,2,4,128]{3,2,1,0:T(4,128)} %qc.3) | copy-start | bytes 36868
  9.9 28.4 %collective-permute-start.2 = (f32[35,8,128]{2,1,0:T(8,128)S(1)}, f32[35,8,128]{2,1,0:T(8,128)S(1)}, u32[]{:S(2)}, u32[]{:S(2)}) collective-permute-start(f32[35,8,128]{2,1,0:T(8,128)S(1)} %get-tuple-element.18), channel_id=1, source_target_pairs={{8,16},{16,8},{24,32},{32,24},{40,48},{48,40},{56,64},{64,56},{72,... | collective-permute-start | bytes 430088 | tf_op jit(solution)/shard_map/ppermute | solution.py:308
  26.2 12.0 %collective-permute-start.3 = (f32[35,8,128]{2,1,0:T(8,128)S(1)}, f32[35,8,128]{2,1,0:T(8,128)S(1)}, u32[]{:S(2)}, u32[]{:S(2)}) collective-permute-start(f32[35,8,128]{2,1,0:T(8,128)S(1)} %get-tuple-element.19), channel_id=1, source_target_pairs={{0,8},{8,0},{16,24},{24,16},{32,40},{40,32},{48,56},{56,48},{64,72... | collective-permute-start | bytes 430088 | tf_op jit(solution)/shard_map/ppermute | solution.py:308

commit v3 on v2

--- a/solution.py
+++ b/solution.py
@@ -9,8 +9,31 @@
 F32 = jnp.float32
 LANES = 128
 
-YT = 44
-XT = 35
+def layout(pieces):
+    table, at = {}, 0
+    for key, rows in pieces:
+        table[key] = (at, rows)
+        at += rows
+    return table, -(-at // 8) * 8
+
+
+X_AT, X_ROWS = layout(
+    [(("f", c, r), 8) for r in (1, 2) for c in range(3)]
+    + [(("f", f, 1), 8) for f in range(3, 8)]
+    + [("bits", 8)]
+    + [(("c", c, x), 4) for c in range(3) for x in range(2)]
+    + [(("c", f, None), 4) for f in range(3, 8)]
+)
+Y_F = (
+    [(("f", c, x), 4) for c in range(3) for x in range(-2, 6)]
+    + [(("bits", side), 4) for side in range(2)]
+    + [(("f", f, x), 2) for f in range(3, 8) for x in range(-1, 5)]
+    + [(("f", 8, x), 2) for x in range(4)]
+)
+Y_C = [(("c", c, x), 2) for c in range(3) for x in range(-2, 4)] + [
+    (("c", f, x), 2) for f in range(3, 8) for x in range(-1, 3)
+]
+Y_AT, Y_ROWS = layout(Y_F + Y_C)
 
 
 def lane_roll(tile, by):
@@ -29,8 +52,9 @@
 
 
 def pre_kernel(uc, pc, mc, muc, lamc, rhoc, qc, omc, uf, pf, mf, muf, lamf, rhof, qf, omf, st, out1, out2, own_f, own_c):
-    even = lax.rem(lax.axis_index("gy"), 2) == 0
+    even = lax.rem(lax.axis_index("gx"), 2) == 0
     eye = lax.broadcasted_iota(jnp.int32, (8, 8), 0) == lax.broadcasted_iota(jnp.int32, (8, 8), 1)
+    lane = lax.broadcasted_iota(jnp.int32, (8, LANES), 1)
 
     def level(u_r, p_r, m_r, mu_r, lam_r, rho_r, q_r, om_r, own, wide):
         for x in range(wide):
@@ -52,12 +76,26 @@
         col = jnp.sum(jnp.where(eye, row, 0.0), axis=1, keepdims=True)
         own_f[32 + x] = 1.0 / jnp.broadcast_to(col, (8, LANES))
 
-    def message(out, up):
-        for k in range(36):
-            out[k] = own_f[k, 4:8] if up else own_f[k, 0:4]
-        for f in range(8):
-            for x in range(2):
-                out[36 + f, 2 * x : 2 * x + 2] = own_c[2 * f + x, 2:4] if up else own_c[2 * f + x, 0:2]
+    def message(out, right):
+        def fine(f, ring):
+            return own_f[4 * f + (4 - ring if right else ring - 1)]
+
+        for key, (at, rows) in X_AT.items():
+            if key[0] == "f":
+                out[at : at + rows] = fine(key[1], key[2])
+            elif key[0] == "c":
+                x = key[2]
+                out[at : at + rows] = own_c[2 * key[1] + ((1 if right else 0) if x is None else x)]
+        bits = jnp.where(lane == 17, fine(8, 1), fine(8, 2))
+        for c in range(3):
+            for r in range(2):
+                to = 4 * c + 2 * r
+                both = jnp.logical_or(lane == to, lane == to + 1)
+                bits = jnp.where(both, lane_roll(fine(c, 3 + r), to + 2), bits)
+        for f in range(3, 8):
+            bits = jnp.where(lane == 9 + f, lane_roll(fine(f, 2), 10 + f), bits)
+        at = X_AT["bits"][0]
+        out[at : at + 8] = bits
 
     @pl.when(even)
     def _():
@@ -70,75 +108,39 @@
         message(out2, True)
 
 
-def mid_kernel(own_f, own_c, r2, r1, ext_f, ext_c, out1, out2):
+def mid_kernel(own_f, own_c, r2, r1, out2, out1):
+    even_x = lax.rem(lax.axis_index("gx"), 2) == 0
     even_y = lax.rem(lax.axis_index("gy"), 2) == 0
-    even_x = lax.rem(lax.axis_index("gx"), 2) == 0
-    for k in range(36):
-        ext_f[k, 0:8] = own_f[k]
-    for k in range(16):
-        ext_c[k, 0:4] = own_c[k]
-
-    def place(above, below):
-        for k in range(36):
-            ext_f[k, 8:12] = above[k]
-            ext_f[k, 12:16] = below[k]
-        for f in range(8):
-            for x in range(2):
-                ext_c[2 * f + x, 4:6] = above[36 + f, 2 * x : 2 * x + 2]
-                ext_c[2 * f + x, 6:8] = below[36 + f, 2 * x : 2 * x + 2]
-
-    @pl.when(even_y)
-    def _():
-        place(r1, r2)
-
-    @pl.when(jnp.logical_not(even_y))
-    def _():
-        place(r2, r1)
-
-    lane = lax.broadcasted_iota(jnp.int32, (16, LANES), 1)
-
-    def message(out, right):
-        def col(ring):
-            return 4 - ring if right else ring - 1
-
-        near = 1 if right else 0
-        for c in range(3):
-            for x in range(2):
-                out[2 * c + x] = ext_c[2 * c + x]
-            out[6 + c] = ext_c[2 * (3 + c) + near]
-        out[9] = ext_c[12 + near]
-        out[10] = ext_c[14 + near]
-
-        def put(k, tile):
-            out[11 + 2 * k] = tile[0:8]
-            out[12 + 2 * k] = tile[8:16]
-
-        for c in range(3):
-            put(c, ext_f[4 * c + col(1)])
-            put(3 + c, ext_f[4 * c + col(2)])
-            put(6 + c, ext_f[4 * (3 + c) + col(1)])
-        put(9, ext_f[24 + col(1)])
-        put(10, ext_f[28 + col(1)])
-        bits = jnp.where(lane == 17, ext_f[32 + col(1)], ext_f[32 + col(2)])
-        for c in range(3):
-            for r in range(2):
-                at = 4 * c + 2 * r
-                both = jnp.logical_or(lane == at, lane == at + 1)
-                bits = jnp.where(both, lane_roll(ext_f[4 * c + col(3 + r)], at + 2), bits)
-            bits = jnp.where(lane == 12 + c, lane_roll(ext_f[4 * (3 + c) + col(2)], 13 + c), bits)
-        bits = jnp.where(lane == 15, lane_roll(ext_f[24 + col(2)], 16), bits)
-        bits = jnp.where(lane == 16, lane_roll(ext_f[28 + col(2)], 17), bits)
-        put(11, bits)
-
-    @pl.when(even_x)
-    def _():
-        message(out1, True)
-        message(out2, False)
-
-    @pl.when(jnp.logical_not(even_x))
-    def _():
-        message(out1, False)
-        message(out2, True)
+
+    def message(out, up, left, right):
+        for key, (at, rows) in Y_AT.items():
+            fine = (8 - rows if up else 0), (8 if up else rows)
+            coarse = (2, 4) if up else (0, 2)
+            if key[0] == "bits":
+                src = X_AT["bits"][0]
+                out[at : at + rows] = (right if key[1] else left)[src + fine[0] : src + fine[1]]
+                continue
+            kind, f, x = key
+            wide = 4 if kind == "f" else 2
+            part = fine if kind == "f" else coarse
+            if 0 <= x < wide:
+                out[at : at + rows] = (own_f if kind == "f" else own_c)[wide * f + x, part[0] : part[1]]
+            else:
+                ring = -x if x < 0 else x - wide + 1
+                if kind == "f":
+                    src = X_AT["f", f, ring][0]
+                else:
+                    src = X_AT["c", f, x % 2 if f < 3 else None][0]
+                out[at : at + rows] = (left if x < 0 else right)[src + part[0] : src + part[1]]
+
+    for y_is_even in (True, False):
+        for x_is_even in (True, False):
+
+            @pl.when(jnp.logical_and(even_x == x_is_even, even_y == y_is_even))
+            def _(y_is_even=y_is_even, x_is_even=x_is_even):
+                left, right = (r2, r1) if x_is_even else (r1, r2)
+                message(out1, y_is_even, left, right)
+                message(out2, not y_is_even, left, right)
 
 
 def operator(w, zp, zm, x, inv_h2, inv_flat, inv_slant, inv_hz2):
@@ -167,19 +169,44 @@
     return lap, grad
 
 
-def post_kernel(ext_f, ext_c, r2, r1, uc, mc, qc, omc, uf, mf, qf, omf, uc_out, uf_out, mc_out, mf_out, halo, scr):
+def post_kernel(
+    own_f, own_c, x2, x1, y2, y1, uc, mc, qc, omc, uf, mf, qf, omf, uc_out, uf_out, mc_out, mf_out, hx, hy, ext_f, ext_c, scr
+):
     gx, gy = lax.axis_index("gx"), lax.axis_index("gy")
     even_x = lax.rem(gx, 2) == 0
-
-    @pl.when(even_x)
-    def _():
-        halo[0] = r2[...]
-        halo[1] = r1[...]
-
-    @pl.when(jnp.logical_not(even_x))
-    def _():
-        halo[0] = r1[...]
-        halo[1] = r2[...]
+    even_y = lax.rem(gy, 2) == 0
+
+    def sides(halo, first, second, even):
+        @pl.when(even)
+        def _():
+            halo[0] = second[...]
+            halo[1] = first[...]
+
+        @pl.when(jnp.logical_not(even))
+        def _():
+            halo[0] = first[...]
+            halo[1] = second[...]
+
+    sides(hx, x1, x2, even_x)
+    sides(hy, y1, y2, even_y)
+
+    index = {}
+
+    def extended(key, own):
+        at, rows = Y_AT[key]
+        if key[0] == "c":
+            ext, tall, far = ext_c, 4, 8
+        else:
+            ext, tall, far = ext_f, 8, 16
+        k = index.setdefault(key, len([i for i in index if (i[0] == "c") == (key[0] == "c")]))
+        ext[k, 0:tall] = own
+        ext[k, tall : tall + rows] = hy[1, at : at + rows]
+        ext[k, far - rows : far] = hy[0, at : at + rows]
+        return ext[k]
+
+    def x_rows(side, key):
+        at, rows = X_AT[key]
+        return hx[side, at : at + rows]
 
     slots = [0]
 
@@ -198,44 +225,44 @@
     keep_left = jnp.where(gx == 0, 0.0, 1.0).astype(F32)
     keep_right = jnp.where(gx == lax.axis_size("gx") - 1, 0.0, 1.0).astype(F32)
 
-    def pair(side, k):
-        return jnp.concatenate([halo[side, 11 + 2 * k], halo[side, 12 + 2 * k]], axis=0)
-
     wf, wc, af, ac, cf, cc, rz = {}, {}, {}, {}, {}, {}, {}
-    for c in range(3):
+
+    def keep(kind, f, x, own):
+        tile = extended((kind, f, x), own)
+        if f < 3:
+            (wf if kind == "f" else wc)[f, x] = tile
+        elif f < 6:
+            (af if kind == "f" else ac)[f - 3, x] = tile
+        elif f < 8:
+            (cf if kind == "f" else cc)[f - 6, x] = tile
+        else:
+            rz[x] = tile
+
+    for f in range(9):
         for x in range(4):
-            wf[c, x] = ext_f[4 * c + x]
-            af[c, x] = ext_f[4 * (3 + c) + x]
+            keep("f", f, x, own_f[4 * f + x])
+    for f in range(8):
         for x in range(2):
-            wc[c, x] = ext_c[2 * c + x]
-            ac[c, x] = ext_c[2 * (3 + c) + x]
-    for t in range(2):
-        for x in range(4):
-            cf[t, x] = ext_f[4 * (6 + t) + x]
-        for x in range(2):
-            cc[t, x] = ext_c[2 * (6 + t) + x]
-    for x in range(4):
-        rz[x] = ext_f[32 + x]
+            keep("c", f, x, own_c[2 * f + x])
     for side in range(2):
 
         def col(ring):
             return 3 + ring if side else -ring
 
-        bits = pair(side, 11)
-        near = 2 if side else -1
-        for c in range(3):
+        for c in range(3):
+            keep("f", c, col(1), x_rows(side, ("f", c, 1)))
+            keep("f", c, col(2), x_rows(side, ("f", c, 2)))
             for x in range(2):
-                wc[c, (2 if side else -2) + x] = halo[side, 2 * c + x]
-            ac[c, near] = halo[side, 6 + c]
-            wf[c, col(1)] = pair(side, c)
-            wf[c, col(2)] = pair(side, 3 + c)
+                keep("c", c, (2 if side else -2) + x, x_rows(side, ("c", c, x)))
+        for f in range(3, 8):
+            keep("f", f, col(1), x_rows(side, ("f", f, 1)))
+            keep("c", f, 2 if side else -1, x_rows(side, ("c", f, None)))
+        bits = extended(("bits", side), x_rows(side, "bits"))
+        for c in range(3):
             for r in range(2):
                 wf[c, col(3 + r)] = lane_roll(bits, 126 - 4 * c - 2 * r)
-            af[c, col(1)] = pair(side, 6 + c)
             af[c, col(2)] = lane_roll(bits, 115 - c)
         for t in range(2):
-            cc[t, near] = halo[side, 9 + t]
-            cf[t, col(1)] = pair(side, 9 + t)
             cf[t, col(2)] = lane_roll(bits, 112 - t)
             rz[col(1 + t)] = jnp.broadcast_to(bits[:, 17 + t : 18 + t], (16, LANES))
 
@@ -344,24 +371,30 @@
     omega_f,
     stretch_f,
 ):
-    up, down, own_f, own_c = call(pre_kernel, [(YT, 4, LANES)] * 2 + [(36, 8, LANES), (16, 4, LANES)], first=True)(
+    out1, out2, own_f, own_c = call(
+        pre_kernel, [(X_ROWS, LANES)] * 2 + [(36, 8, LANES), (16, 4, LANES)], first=True
+    )(
         u_now_c, u_prev_c, memory_c, mu_c, lam_c, rho_c, q_c, omega_c,
         u_now_f, u_prev_f, memory_f, mu_f, lam_f, rho_f, q_f, omega_f, stretch_f,
     )
-    r2 = swap(down, "gy", 1)
-    r1 = swap(up, "gy", 0)
-    ext_f, ext_c, right, left = call(mid_kernel, [(36, 16, LANES), (16, 8, LANES)] + [(XT, 8, LANES)] * 2)(
-        own_f, own_c, r2, r1
-    )
-    s2 = swap(left, "gx", 1)
-    s1 = swap(right, "gx", 0)
+    x2 = swap(out2, "gx", 1)
+    x1 = swap(out1, "gx", 0)
+    out2, out1 = call(mid_kernel, [(Y_ROWS, LANES)] * 2)(own_f, own_c, x2, x1)
+    y2 = swap(out2, "gy", 1)
+    y1 = swap(out1, "gy", 0)
     return tuple(
         call(
             post_kernel,
             [u_now_c.shape, u_now_f.shape, memory_c.shape, memory_f.shape],
-            [pltpu.VMEM((2, XT, 8, LANES), F32), pltpu.VMEM((SCRATCH, 16, LANES), F32)],
+            [
+                pltpu.VMEM((2, X_ROWS, LANES), F32),
+                pltpu.VMEM((2, Y_ROWS, LANES), F32),
+                pltpu.VMEM((len(Y_F), 16, LANES), F32),
+                pltpu.VMEM((len(Y_C), 8, LANES), F32),
+                pltpu.VMEM((SCRATCH, 16, LANES), F32),
+            ],
             last=True,
-        )(ext_f, ext_c, s2, s1, u_now_c, memory_c, q_c, omega_c, u_now_f, memory_f, q_f, omega_f)
+        )(own_f, own_c, x2, x1, y2, y1, u_now_c, memory_c, q_c, omega_c, u_now_f, memory_f, q_f, omega_f)
     )
 
 

time: 40.3 us -> 34.6 us (0.86); the launches traced: 39.6 us -> 34.4 us
  waiting for transfers between devices: 11.4 us -> 4.48 us
  starting transfers between devices: 24.7 us -> 26.3 us
    ppermute x4, waiting for transfers between devices: 11.4 us -> 4.48 us  [swap(): return lax.ppermute(value, axis, pairs)]
    ppermute x4, starting transfers between devices: 24.7 us -> 26.3 us  [swap(): return lax.ppermute(value, axis, pairs)]
  transfers between devices with their start and end apart: 4 -> 4, of which waited for: 3 -> 4; matrix products, arithmetic and copies ran while one was open for 0% -> 0% of each run, Pallas kernels for 0% -> 0%
where the time goes in v3:
time: 34.6 us; the launch traced here: 34.4 us
  starting transfers between devices  26.3 us (76%)
  waiting for transfers between devices  4.48 us (13%)
  Pallas kernels  2.74 us (8%)
  between operations  0.76 us (2%)
    ppermute x4, starting transfers between devices, swap(): return lax.ppermute(value, axis, pairs)  26.3 us
    ppermute x4, waiting for transfers between devices, swap(): return lax.ppermute(value, axis, pairs)  4.48 us
    pallas_call x3, Pallas kernels, run(): pl.pallas_call(kernel, out_shape=[(jax.ShapeDtypeStruct if last else pltp...  2.74 us
  transfers between devices with their start and end apart: 4, of which 4 were waited for; matrix products, arithmetic and copies ran while one was open for 0% of the time, Pallas kernels for 0%

profile of v3, /device:TPU:57, one launch (start us, length us, event | category | flops | bytes accessed | tf_op | source)
XLA Modules:
  0.0 34.4 jit_solution(15474247792652470588)
XLA Ops:
  0.6 0.0 copy-start.4
  0.6 0.0 copy-start.7
  0.7 1.3 %shard_map.192 = (f32[144,128]{1,0:T(8,128)S(1)}, f32[144,128]{1,0:T(8,128)S(1)}, f32[36,8,128]{2,1,0:T(8,128)S(1)}, f32[16,4,128]{2,1,0:T(4,128)S(1)}) custom-call(f32[3,2,4,128]{3,2,1,0:T(4,128)} %uc.3, f32[3,2,4,128]{3,2,1,0:T(4,128)} %pc.1, f32[3,3,2,4,128]{4,3,2,1,0:T(4,128)} %mc.3, f32[2,4,128]{2,1,0:T(4,128)} %muc.1, f32[2,4,128]{2,1,0:T(4,128)} %lamc.1, ...), custom_call_target="tpu_custom_call" | custom-call | tf_op jit(solution)/shard_map/pallas_call | solution.py:344
  1.9 17.3 %collective-permute-start = (f32[144,128]{1,0:T(8,128)S(1)}, f32[144,128]{1,0:T(8,128)S(1)}, u32[]{:S(2)}, u32[]{:S(2)}) collective-permute-start(f32[144,128]{1,0:T(8,128)S(1)} %get-tuple-element.12), channel_id=1, source_target_pairs={{8,16},{16,8},{24,32},{32,24},{40,48},{48,40},{56,64},{64,56},{72,... | collective-permute-start | bytes 221192 | tf_op jit(solution)/shard_map/ppermute | solution.py:335
  19.2 1.9 %collective-permute-start.1 = (f32[144,128]{1,0:T(8,128)S(1)}, f32[144,128]{1,0:T(8,128)S(1)}, u32[]{:S(2)}, u32[]{:S(2)}) collective-permute-start(f32[144,128]{1,0:T(8,128)S(1)} %get-tuple-element.13), channel_id=1, source_target_pairs={{0,8},{8,0},{16,24},{24,16},{32,40},{40,32},{48,56},{56,48},{64,72... | collective-permute-start | bytes 221192 | tf_op jit(solution)/shard_map/ppermute | solution.py:335
  21.2 0.1 collective-permute-done.r2.x2
  21.2 3.1 %collective-permute-done.1.r1.x1 = f32[144,128]{1,0:T(8,128)S(1)} collective-permute-done((f32[144,128]{1,0:T(8,128)S(1)}, f32[144,128]{1,0:T(8,128)S(1)}, u32[]{:S(2)}, u32[]{:S(2)}) %collective-permute-start.1) | collective-permute-done | bytes 73760 | tf_op jit(solution)/shard_map/ppermute | solution.py:335
  24.3 0.0 copy-start
  24.3 0.0 copy-start.1
  24.3 0.0 copy-start.2
  24.3 0.0 copy-start.3
  24.3 0.0 copy-start.5
  24.4 0.0 copy-start.6
  24.4 0.1 shard_map.193
  24.5 5.2 %collective-permute-start.2 = (f32[248,128]{1,0:T(8,128)S(1)}, f32[248,128]{1,0:T(8,128)S(1)}, u32[]{:S(2)}, u32[]{:S(2)}) collective-permute-start(f32[248,128]{1,0:T(8,128)S(1)} %get-tuple-element.14), channel_id=1, source_target_pairs={{1,2},{2,1},{3,4},{4,3},{5,6},{6,5},{9,10},{10,9},{11,12},{12,11},... | collective-permute-start | bytes 380936 | tf_op jit(solution)/shard_map/ppermute | solution.py:335
  29.7 1.9 %collective-permute-start.3 = (f32[248,128]{1,0:T(8,128)S(1)}, f32[248,128]{1,0:T(8,128)S(1)}, u32[]{:S(2)}, u32[]{:S(2)}) collective-permute-start(f32[248,128]{1,0:T(8,128)S(1)} %get-tuple-element.15), channel_id=1, source_target_pairs={{0,1},{1,0},{2,3},{3,2},{4,5},{5,4},{6,7},{7,6},{8,9},{9,8},{10,11... | collective-permute-start | bytes 380936 | tf_op jit(solution)/shard_map/ppermute | solution.py:335
  31.6 0.7 %collective-permute-done.2.y2 = f32[248,128]{1,0:T(8,128)S(1)} collective-permute-done((f32[248,128]{1,0:T(8,128)S(1)}, f32[248,128]{1,0:T(8,128)S(1)}, u32[]{:S(2)}, u32[]{:S(2)}) %collective-permute-start.2) | collective-permute-done | bytes 127008 | tf_op jit(solution)/shard_map/ppermute | solution.py:335
  32.3 0.6 %collective-permute-done.3.y1 = f32[248,128]{1,0:T(8,128)S(1)} collective-permute-done((f32[248,128]{1,0:T(8,128)S(1)}, f32[248,128]{1,0:T(8,128)S(1)}, u32[]{:S(2)}, u32[]{:S(2)}) %collective-permute-start.3) | collective-permute-done | bytes 127008 | tf_op jit(solution)/shard_map/ppermute | solution.py:335
  32.9 0.0 copy-done.4
  32.9 0.0 copy-done.7
  33.0 0.0 copy-done
  33.0 0.0 copy-done.1
  33.0 0.0 copy-done.2
  33.0 0.0 copy-done.3
  33.0 0.0 copy-done.5
  33.0 0.0 copy-done.6
  33.0 1.3 %shard_map.194 = (f32[3,2,4,128]{3,2,1,0:T(4,128)}, f32[3,4,8,128]{3,2,1,0:T(8,128)}, f32[3,3,2,4,128]{4,3,2,1,0:T(4,128)}, f32[3,3,4,8,128]{4,3,2,1,0:T(8,128)}) custom-call(f32[36,8,128]{2,1,0:T(8,128)S(1)} %get-tuple-element.10.own_f, f32[16,4,128]{2,1,0:T(4,128)S(1)} %get-tuple-element.11.own_c, f32[144,128]{1,0:T(8,128)S(1)} %collective-permute-done.r2.x2, ...), custom_call_target="tpu_custom_call" | custom-call | tf_op jit(solution)/shard_map/pallas_call | solution.py:344
Async XLA Ops:
  0.6 32.3 %copy-start.4 = (f32[3,3,2,4,128]{4,3,2,1,0:T(4,128)S(1)}, f32[3,3,2,4,128]{4,3,2,1,0:T(4,128)}, u32[]{:S(2)}) copy-start(f32[3,3,2,4,128]{4,3,2,1,0:T(4,128)} %mc.3) | copy-start | bytes 110596
  0.6 32.3 %copy-start.7 = (f32[3,2,4,128]{3,2,1,0:T(4,128)S(1)}, f32[3,2,4,128]{3,2,1,0:T(4,128)}, u32[]{:S(2)}) copy-start(f32[3,2,4,128]{3,2,1,0:T(4,128)} %omc.3) | copy-start | bytes 36868
  1.9 19.3 %collective-permute-start = (f32[144,128]{1,0:T(8,128)S(1)}, f32[144,128]{1,0:T(8,128)S(1)}, u32[]{:S(2)}, u32[]{:S(2)}) collective-permute-start(f32[144,128]{1,0:T(8,128)S(1)} %get-tuple-element.12), channel_id=1, source_target_pairs={{8,16},{16,8},{24,32},{32,24},{40,48},{48,40},{56,64},{64,56},{72,... | collective-permute-start | bytes 221192 | tf_op jit(solution)/shard_map/ppermute | solution.py:335
  19.2 5.1 %collective-permute-start.1 = (f32[144,128]{1,0:T(8,128)S(1)}, f32[144,128]{1,0:T(8,128)S(1)}, u32[]{:S(2)}, u32[]{:S(2)}) collective-permute-start(f32[144,128]{1,0:T(8,128)S(1)} %get-tuple-element.13), channel_id=1, source_target_pairs={{0,8},{8,0},{16,24},{24,16},{32,40},{40,32},{48,56},{56,48},{64,72... | collective-permute-start | bytes 221192 | tf_op jit(solution)/shard_map/ppermute | solution.py:335
  24.3 8.6 %copy-start = (f32[3,3,4,8,128]{4,3,2,1,0:T(8,128)S(1)}, f32[3,3,4,8,128]{4,3,2,1,0:T(8,128)}, u32[]{:S(2)}) copy-start(f32[3,3,4,8,128]{4,3,2,1,0:T(8,128)} %mf.3) | copy-start | bytes 442372
  24.3 8.6 %copy-start.1 = (f32[3,4,8,128]{3,2,1,0:T(8,128)S(1)}, f32[3,4,8,128]{3,2,1,0:T(8,128)}, u32[]{:S(2)}) copy-start(f32[3,4,8,128]{3,2,1,0:T(8,128)} %uf.3) | copy-start | bytes 147460
  24.3 8.6 %copy-start.2 = (f32[3,4,8,128]{3,2,1,0:T(8,128)S(1)}, f32[3,4,8,128]{3,2,1,0:T(8,128)}, u32[]{:S(2)}) copy-start(f32[3,4,8,128]{3,2,1,0:T(8,128)} %qf.3) | copy-start | bytes 147460
  24.3 8.6 %copy-start.3 = (f32[3,4,8,128]{3,2,1,0:T(8,128)S(1)}, f32[3,4,8,128]{3,2,1,0:T(8,128)}, u32[]{:S(2)}) copy-start(f32[3,4,8,128]{3,2,1,0:T(8,128)} %omf.3) | copy-start | bytes 147460
  24.3 8.6 %copy-start.5 = (f32[3,2,4,128]{3,2,1,0:T(4,128)S(1)}, f32[3,2,4,128]{3,2,1,0:T(4,128)}, u32[]{:S(2)}) copy-start(f32[3,2,4,128]{3,2,1,0:T(4,128)} %uc.3) | copy-start | bytes 36868
  24.4 8.6 %copy-start.6 = (f32[3,2,4,128]{3,2,1,0:T(4,128)S(1)}, f32[3,2,4,128]{3,2,1,0:T(4,128)}, u32[]{:S(2)}) copy-start(f32[3,2,4,128]{3,2,1,0:T(4,128)} %qc.3) | copy-start | bytes 36868
  24.5 7.8 %collective-permute-start.2 = (f32[248,128]{1,0:T(8,128)S(1)}, f32[248,128]{1,0:T(8,128)S(1)}, u32[]{:S(2)}, u32[]{:S(2)}) collective-permute-start(f32[248,128]{1,0:T(8,128)S(1)} %get-tuple-element.14), channel_id=1, source_target_pairs={{1,2},{2,1},{3,4},{4,3},{5,6},{6,5},{9,10},{10,9},{11,12},{12,11},... | collective-permute-start | bytes 380936 | tf_op jit(solution)/shard_map/ppermute | solution.py:335
  29.7 3.2 %collective-permute-start.3 = (f32[248,128]{1,0:T(8,128)S(1)}, f32[248,128]{1,0:T(8,128)S(1)}, u32[]{:S(2)}, u32[]{:S(2)}) collective-permute-start(f32[248,128]{1,0:T(8,128)S(1)} %get-tuple-element.15), channel_id=1, source_target_pairs={{0,1},{1,0},{2,3},{3,2},{4,5},{5,4},{6,7},{7,6},{8,9},{9,8},{10,11... | collective-permute-start | bytes 380936 | tf_op jit(solution)/shard_map/ppermute | solution.py:335

commit v4 on v3

--- a/solution.py
+++ b/solution.py
@@ -51,8 +51,9 @@
     return old, nxt, new
 
 
-def pre_kernel(uc, pc, mc, muc, lamc, rhoc, qc, omc, uf, pf, mf, muf, lamf, rhof, qf, omf, st, out1, out2, own_f, own_c):
+def pre_kernel(uc, pc, mc, muc, lamc, rhoc, qc, omc, uf, pf, mf, muf, lamf, rhof, qf, omf, st, out1, out2, out3, own_f, own_c):
     even = lax.rem(lax.axis_index("gx"), 2) == 0
+    outer_first = far_first(lax.axis_index("gy"))
     eye = lax.broadcasted_iota(jnp.int32, (8, 8), 0) == lax.broadcasted_iota(jnp.int32, (8, 8), 1)
     lane = lax.broadcasted_iota(jnp.int32, (8, LANES), 1)
 
@@ -97,28 +98,36 @@
         at = X_AT["bits"][0]
         out[at : at + 8] = bits
 
-    @pl.when(even)
-    def _():
-        message(out1, True)
-        message(out2, False)
-
-    @pl.when(jnp.logical_not(even))
-    def _():
-        message(out1, False)
-        message(out2, True)
-
-
-def mid_kernel(own_f, own_c, r2, r1, out2, out1):
-    even_x = lax.rem(lax.axis_index("gx"), 2) == 0
-    even_y = lax.rem(lax.axis_index("gy"), 2) == 0
-
-    def message(out, up, left, right):
+    for is_even in (True, False):
+        for is_first in (True, False):
+
+            @pl.when(jnp.logical_and(even == is_even, outer_first == is_first))
+            def _(is_even=is_even, is_first=is_first):
+                message(out1 if is_first else out2, not is_even)
+                message(out2 if is_first else out1, is_even)
+                message(out3, not is_even)
+
+
+def mid_kernel(own_f, own_c, r1, r2, r3, out2, out1, halo):
+    gx, gy = lax.axis_index("gx"), lax.axis_index("gy")
+    even_x = lax.rem(gx, 2) == 0
+    even_y = lax.rem(gy, 2) == 0
+    inner_at = jnp.where(far_first(gy), 1, 0)
+    outer_at = jnp.where(late(gx), 2, 1 - inner_at)
+    for side, at in ((0, jnp.where(even_x, outer_at, inner_at)), (1, jnp.where(even_x, inner_at, outer_at))):
+        for k, r in enumerate((r1, r2, r3)):
+
+            @pl.when(at == k)
+            def _(side=side, r=r):
+                halo[side] = r[...]
+
+    def message(out, up):
         for key, (at, rows) in Y_AT.items():
             fine = (8 - rows if up else 0), (8 if up else rows)
             coarse = (2, 4) if up else (0, 2)
             if key[0] == "bits":
                 src = X_AT["bits"][0]
-                out[at : at + rows] = (right if key[1] else left)[src + fine[0] : src + fine[1]]
+                out[at : at + rows] = halo[key[1], src + fine[0] : src + fine[1]]
                 continue
             kind, f, x = key
             wide = 4 if kind == "f" else 2
@@ -131,16 +140,17 @@
                     src = X_AT["f", f, ring][0]
                 else:
                     src = X_AT["c", f, x % 2 if f < 3 else None][0]
-                out[at : at + rows] = (left if x < 0 else right)[src + part[0] : src + part[1]]
-
-    for y_is_even in (True, False):
-        for x_is_even in (True, False):
-
-            @pl.when(jnp.logical_and(even_x == x_is_even, even_y == y_is_even))
-            def _(y_is_even=y_is_even, x_is_even=x_is_even):
-                left, right = (r2, r1) if x_is_even else (r1, r2)
-                message(out1, y_is_even, left, right)
-                message(out2, not y_is_even, left, right)
+                out[at : at + rows] = halo[0 if x < 0 else 1, src + part[0] : src + part[1]]
+
+    @pl.when(even_y)
+    def _():
+        message(out1, True)
+        message(out2, False)
+
+    @pl.when(jnp.logical_not(even_y))
+    def _():
+        message(out1, False)
+        message(out2, True)
 
 
 def operator(w, zp, zm, x, inv_h2, inv_flat, inv_slant, inv_hz2):
@@ -170,10 +180,9 @@
 
 
 def post_kernel(
-    own_f, own_c, x2, x1, y2, y1, uc, mc, qc, omc, uf, mf, qf, omf, uc_out, uf_out, mc_out, mf_out, hx, hy, ext_f, ext_c, scr
+    own_f, own_c, hx, y2, y1, uc, mc, qc, omc, uf, mf, qf, omf, uc_out, uf_out, mc_out, mf_out, hy, ext_f, ext_c, scr
 ):
     gx, gy = lax.axis_index("gx"), lax.axis_index("gy")
-    even_x = lax.rem(gx, 2) == 0
     even_y = lax.rem(gy, 2) == 0
 
     def sides(halo, first, second, even):
@@ -187,7 +196,6 @@
             halo[0] = first[...]
             halo[1] = second[...]
 
-    sides(hx, x1, x2, even_x)
     sides(hy, y1, y2, even_y)
 
     index = {}
@@ -326,6 +334,33 @@
 
 
 SCRATCH = 3 * (10 + 6 + 6 + 4)
+
+
+X_RUN, SEAM = 4, 12
+
+
+def late(gx):
+    at = gx % SEAM
+    if isinstance(gx, int):
+        return at == SEAM - 1 or (at != 0 and at % X_RUN == 0)
+    return jnp.logical_or(at == SEAM - 1, jnp.logical_and(at != 0, lax.rem(at, X_RUN) == 0))
+
+
+def far_first(gy):
+    return gy < -(-5 * lax.axis_size("gy") // 8)
+
+
+def x_exchange(first, second, third):
+    nx, ny = lax.axis_size("gx"), lax.axis_size("gy")
+    pairs = [[], [], []]
+    for i in range(nx - 1):
+        for j in range(ny):
+            outer = i % 2 == 1
+            turn = 0 if outer == far_first(j) else 1
+            for source, target in ((i, i + 1), (i + 1, i)):
+                held = outer and i % X_RUN == X_RUN - 1 and late(target)
+                pairs[2 if held else turn].append((source * ny + j, target * ny + j))
+    return [lax.ppermute(v, ("gx", "gy"), p) for v, p in zip((first, second, third), pairs)]
 
 
 def swap(value, axis, first):
@@ -371,15 +406,15 @@
     omega_f,
     stretch_f,
 ):
-    out1, out2, own_f, own_c = call(
-        pre_kernel, [(X_ROWS, LANES)] * 2 + [(36, 8, LANES), (16, 4, LANES)], first=True
+    out1, out2, out3, own_f, own_c = call(
+        pre_kernel, [(X_ROWS, LANES)] * 3 + [(36, 8, LANES), (16, 4, LANES)], first=True
     )(
         u_now_c, u_prev_c, memory_c, mu_c, lam_c, rho_c, q_c, omega_c,
         u_now_f, u_prev_f, memory_f, mu_f, lam_f, rho_f, q_f, omega_f, stretch_f,
     )
-    x2 = swap(out2, "gx", 1)
-    x1 = swap(out1, "gx", 0)
-    out2, out1 = call(mid_kernel, [(Y_ROWS, LANES)] * 2)(own_f, own_c, x2, x1)
+    out2, out1, halo = call(mid_kernel, [(Y_ROWS, LANES)] * 2 + [(2, X_ROWS, LANES)])(
+        own_f, own_c, *x_exchange(out1, out2, out3)
+    )
     y2 = swap(out2, "gy", 1)
     y1 = swap(out1, "gy", 0)
     return tuple(
@@ -387,14 +422,13 @@
             post_kernel,
             [u_now_c.shape, u_now_f.shape, memory_c.shape, memory_f.shape],
             [
-                pltpu.VMEM((2, X_ROWS, LANES), F32),
                 pltpu.VMEM((2, Y_ROWS, LANES), F32),
                 pltpu.VMEM((len(Y_F), 16, LANES), F32),
                 pltpu.VMEM((len(Y_C), 8, LANES), F32),
                 pltpu.VMEM((SCRATCH, 16, LANES), F32),
             ],
             last=True,
-        )(own_f, own_c, x2, x1, y2, y1, u_now_c, memory_c, q_c, omega_c, u_now_f, memory_f, q_f, omega_f)
+        )(own_f, own_c, halo, y2, y1, u_now_c, memory_c, q_c, omega_c, u_now_f, memory_f, q_f, omega_f)
     )
 
 

time: 34.6 us -> 37.6 us (1.087)
  starting transfers between devices: 26.3 us -> 31.1 us
  waiting for transfers between devices: 4.48 us -> 2.68 us
    ppermute x0 -> x3, starting transfers between devices: none -> 21.9 us  [x_exchange(): lax.ppermute(v, ('gx', 'gy'), p)]
    ppermute x4 -> x2, starting transfers between devices: 26.3 us -> 9.18 us  [swap(): return lax.ppermute(value, axis, pairs)]
    ppermute x4 -> x2, waiting for transfers between devices: 4.48 us -> 1.31 us  [swap(): return lax.ppermute(value, axis, pairs)]
    ppermute x0 -> x3, waiting for transfers between devices: none -> 1.37 us  [x_exchange(): lax.ppermute(v, ('gx', 'gy'), p)]
  transfers between devices with their start and end apart: 4 -> 5, of which waited for: 4 -> 3; matrix products, arithmetic and copies ran while one was open for 0% -> 0% of each run, Pallas kernels for 0% -> 0%
where the time goes in v4:
time: 37.6 us; the launch traced here: 37.3 us
  starting transfers between devices  31.1 us (83%)
  Pallas kernels  2.78 us (7%)
  waiting for transfers between devices  2.68 us (7%)
  between operations  0.78 us (2%)
    ppermute x3, starting transfers between devices, x_exchange(): lax.ppermute(v, ('gx', 'gy'), p)  21.9 us
    ppermute x2, starting transfers between devices, swap(): return lax.ppermute(value, axis, pairs)  9.18 us
    pallas_call x3, Pallas kernels, run(): pl.pallas_call(kernel, out_shape=[(jax.ShapeDtypeStruct if last else pltp...  2.78 us
    ppermute x3, waiting for transfers between devices, x_exchange(): lax.ppermute(v, ('gx', 'gy'), p)  1.37 us
    ppermute x2, waiting for transfers between devices, swap(): return lax.ppermute(value, axis, pairs)  1.31 us
  transfers between devices with their start and end apart: 5, of which 3 were waited for; matrix products, arithmetic and copies ran while one was open for 0% of the time, Pallas kernels for 0%

profile of v4, /device:TPU:57, one launch (start us, length us, event | category | flops | bytes accessed | tf_op | source)
XLA Modules:
  0.0 37.3 jit_solution(14868139947930185934)
XLA Ops:
  0.6 1.3 %shard_map.192 = (f32[144,128]{1,0:T(8,128)S(1)}, f32[144,128]{1,0:T(8,128)S(1)}, f32[144,128]{1,0:T(8,128)S(1)}, f32[36,8,128]{2,1,0:T(8,128)S(1)}, f32[16,4,128]{2,1,0:T(4,128)S(1)}) custom-call(f32[3,2,4,128]{3,2,1,0:T(4,128)} %uc.3, f32[3,2,4,128]{3,2,1,0:T(4,128)} %pc.1, f32[3,3,2,4,128]{4,3,2,1,0:T(4,128)} %mc.3, f32[2,4,128]{2,1,0:T(4,128)} %muc.1, ...), custom_call_target="tpu_custom_call" | custom-call | tf_op jit(solution)/shard_map/pallas_call | solution.py:379
  2.0 1.3 %collective-permute-start = (f32[144,128]{1,0:T(8,128)S(1)}, f32[144,128]{1,0:T(8,128)S(1)}, u32[]{:S(2)}, u32[]{:S(2)}) collective-permute-start(f32[144,128]{1,0:T(8,128)S(1)} %get-tuple-element.14), channel_id=1, source_target_pairs={{5,13},{13,5},{6,14},{14,6},{7,15},{15,7},{8,16},{16,8},{9,17},{17... | collective-permute-start | bytes 221192 | tf_op jit(solution)/shard_map/ppermute | solution.py:363
  3.3 4.9 %collective-permute-start.1 = (f32[144,128]{1,0:T(8,128)S(1)}, f32[144,128]{1,0:T(8,128)S(1)}, u32[]{:S(2)}, u32[]{:S(2)}) collective-permute-start(f32[144,128]{1,0:T(8,128)S(1)} %get-tuple-element.15), channel_id=1, source_target_pairs={{0,8},{8,0},{1,9},{9,1},{2,10},{10,2},{3,11},{11,3},{4,12},{12,4},... | collective-permute-start | bytes 221192 | tf_op jit(solution)/shard_map/ppermute | solution.py:363
  8.2 15.6 %collective-permute-start.2 = (f32[144,128]{1,0:T(8,128)S(1)}, f32[144,128]{1,0:T(8,128)S(1)}, u32[]{:S(2)}, u32[]{:S(2)}) collective-permute-start(f32[144,128]{1,0:T(8,128)S(1)} %get-tuple-element.16), channel_id=1, source_target_pairs={{24,32},{25,33},{26,34},{27,35},{28,36},{29,37},{30,38},{31,39},{5... | collective-permute-start | bytes 221192 | tf_op jit(solution)/shard_map/ppermute | solution.py:363
  23.9 0.0 collective-permute-done.r1
  23.9 0.0 collective-permute-done.1.r2
  23.9 1.4 %collective-permute-done.2.r3 = f32[144,128]{1,0:T(8,128)S(1)} collective-permute-done((f32[144,128]{1,0:T(8,128)S(1)}, f32[144,128]{1,0:T(8,128)S(1)}, u32[]{:S(2)}, u32[]{:S(2)}) %collective-permute-start.2) | collective-permute-done | bytes 73760 | tf_op jit(solution)/shard_map/ppermute | solution.py:363
  25.3 0.0 copy-start
  25.3 0.0 copy-start.1
  25.3 0.0 copy-start.2
  25.3 0.0 copy-start.3
  25.3 0.0 copy-start.4
  25.3 0.0 copy-start.5
  25.3 0.0 copy-start.6
  25.3 0.0 copy-start.7
  25.3 0.1 shard_map.193
  25.5 7.3 %collective-permute-start.3 = (f32[248,128]{1,0:T(8,128)S(1)}, f32[248,128]{1,0:T(8,128)S(1)}, u32[]{:S(2)}, u32[]{:S(2)}) collective-permute-start(f32[248,128]{1,0:T(8,128)S(1)} %get-tuple-element.18), channel_id=1, source_target_pairs={{1,2},{2,1},{3,4},{4,3},{5,6},{6,5},{9,10},{10,9},{11,12},{12,11},... | collective-permute-start | bytes 380936 | tf_op jit(solution)/shard_map/ppermute | solution.py:370
  32.7 1.9 %collective-permute-start.4 = (f32[248,128]{1,0:T(8,128)S(1)}, f32[248,128]{1,0:T(8,128)S(1)}, u32[]{:S(2)}, u32[]{:S(2)}) collective-permute-start(f32[248,128]{1,0:T(8,128)S(1)} %get-tuple-element.19), channel_id=1, source_target_pairs={{0,1},{1,0},{2,3},{3,2},{4,5},{5,4},{6,7},{7,6},{8,9},{9,8},{10,11... | collective-permute-start | bytes 380936 | tf_op jit(solution)/shard_map/ppermute | solution.py:370
  34.7 0.7 %collective-permute-done.3.y2 = f32[248,128]{1,0:T(8,128)S(1)} collective-permute-done((f32[248,128]{1,0:T(8,128)S(1)}, f32[248,128]{1,0:T(8,128)S(1)}, u32[]{:S(2)}, u32[]{:S(2)}) %collective-permute-start.3) | collective-permute-done | bytes 127008 | tf_op jit(solution)/shard_map/ppermute | solution.py:370
  35.3 0.6 %collective-permute-done.4.y1 = f32[248,128]{1,0:T(8,128)S(1)} collective-permute-done((f32[248,128]{1,0:T(8,128)S(1)}, f32[248,128]{1,0:T(8,128)S(1)}, u32[]{:S(2)}, u32[]{:S(2)}) %collective-permute-start.4) | collective-permute-done | bytes 127008 | tf_op jit(solution)/shard_map/ppermute | solution.py:370
  36.0 0.0 copy-done
  36.0 0.0 copy-done.1
  36.0 0.0 copy-done.2
  36.0 0.0 copy-done.3
  36.0 0.0 copy-done.4
  36.0 0.0 copy-done.5
  36.0 0.0 copy-done.6
  36.0 0.0 copy-done.7
  36.0 1.3 %shard_map.194 = (f32[3,2,4,128]{3,2,1,0:T(4,128)}, f32[3,4,8,128]{3,2,1,0:T(8,128)}, f32[3,3,2,4,128]{4,3,2,1,0:T(4,128)}, f32[3,3,4,8,128]{4,3,2,1,0:T(8,128)}) custom-call(f32[36,8,128]{2,1,0:T(8,128)S(1)} %get-tuple-element.12.own_f, f32[16,4,128]{2,1,0:T(4,128)S(1)} %get-tuple-element.13.own_c, f32[2,144,128]{2,1,0:T(8,128)S(1)} %get-tuple-element.17.hx, ...), custom_call_target="tpu_custom_call" | custom-call | tf_op jit(solution)/shard_map/pallas_call | solution.py:379
Async XLA Ops:
  2.0 21.9 %collective-permute-start = (f32[144,128]{1,0:T(8,128)S(1)}, f32[144,128]{1,0:T(8,128)S(1)}, u32[]{:S(2)}, u32[]{:S(2)}) collective-permute-start(f32[144,128]{1,0:T(8,128)S(1)} %get-tuple-element.14), channel_id=1, source_target_pairs={{5,13},{13,5},{6,14},{14,6},{7,15},{15,7},{8,16},{16,8},{9,17},{17... | collective-permute-start | bytes 221192 | tf_op jit(solution)/shard_map/ppermute | solution.py:363
  3.3 20.6 %collective-permute-start.1 = (f32[144,128]{1,0:T(8,128)S(1)}, f32[144,128]{1,0:T(8,128)S(1)}, u32[]{:S(2)}, u32[]{:S(2)}) collective-permute-start(f32[144,128]{1,0:T(8,128)S(1)} %get-tuple-element.15), channel_id=1, source_target_pairs={{0,8},{8,0},{1,9},{9,1},{2,10},{10,2},{3,11},{11,3},{4,12},{12,4},... | collective-permute-start | bytes 221192 | tf_op jit(solution)/shard_map/ppermute | solution.py:363
  8.2 17.0 %collective-permute-start.2 = (f32[144,128]{1,0:T(8,128)S(1)}, f32[144,128]{1,0:T(8,128)S(1)}, u32[]{:S(2)}, u32[]{:S(2)}) collective-permute-start(f32[144,128]{1,0:T(8,128)S(1)} %get-tuple-element.16), channel_id=1, source_target_pairs={{24,32},{25,33},{26,34},{27,35},{28,36},{29,37},{30,38},{31,39},{5... | collective-permute-start | bytes 221192 | tf_op jit(solution)/shard_map/ppermute | solution.py:363
  25.3 10.7 %copy-start = (f32[3,3,4,8,128]{4,3,2,1,0:T(8,128)S(1)}, f32[3,3,4,8,128]{4,3,2,1,0:T(8,128)}, u32[]{:S(2)}) copy-start(f32[3,3,4,8,128]{4,3,2,1,0:T(8,128)} %mf.3) | copy-start | bytes 442372
  25.3 10.7 %copy-start.1 = (f32[3,4,8,128]{3,2,1,0:T(8,128)S(1)}, f32[3,4,8,128]{3,2,1,0:T(8,128)}, u32[]{:S(2)}) copy-start(f32[3,4,8,128]{3,2,1,0:T(8,128)} %uf.3) | copy-start | bytes 147460
  25.3 10.7 %copy-start.2 = (f32[3,4,8,128]{3,2,1,0:T(8,128)S(1)}, f32[3,4,8,128]{3,2,1,0:T(8,128)}, u32[]{:S(2)}) copy-start(f32[3,4,8,128]{3,2,1,0:T(8,128)} %qf.3) | copy-start | bytes 147460
  25.3 10.7 %copy-start.3 = (f32[3,4,8,128]{3,2,1,0:T(8,128)S(1)}, f32[3,4,8,128]{3,2,1,0:T(8,128)}, u32[]{:S(2)}) copy-start(f32[3,4,8,128]{3,2,1,0:T(8,128)} %omf.3) | copy-start | bytes 147460
  25.3 10.7 %copy-start.4 = (f32[3,3,2,4,128]{4,3,2,1,0:T(4,128)S(1)}, f32[3,3,2,4,128]{4,3,2,1,0:T(4,128)}, u32[]{:S(2)}) copy-start(f32[3,3,2,4,128]{4,3,2,1,0:T(4,128)} %mc.3) | copy-start | bytes 110596
  25.3 10.7 %copy-start.5 = (f32[3,2,4,128]{3,2,1,0:T(4,128)S(1)}, f32[3,2,4,128]{3,2,1,0:T(4,128)}, u32[]{:S(2)}) copy-start(f32[3,2,4,128]{3,2,1,0:T(4,128)} %uc.3) | copy-start | bytes 36868
  25.3 10.7 %copy-start.6 = (f32[3,2,4,128]{3,2,1,0:T(4,128)S(1)}, f32[3,2,4,128]{3,2,1,0:T(4,128)}, u32[]{:S(2)}) copy-start(f32[3,2,4,128]{3,2,1,0:T(4,128)} %qc.3) | copy-start | bytes 36868
  25.3 10.7 %copy-start.7 = (f32[3,2,4,128]{3,2,1,0:T(4,128)S(1)}, f32[3,2,4,128]{3,2,1,0:T(4,128)}, u32[]{:S(2)}) copy-start(f32[3,2,4,128]{3,2,1,0:T(4,128)} %omc.3) | copy-start | bytes 36868
  25.5 9.9 %collective-permute-start.3 = (f32[248,128]{1,0:T(8,128)S(1)}, f32[248,128]{1,0:T(8,128)S(1)}, u32[]{:S(2)}, u32[]{:S(2)}) collective-permute-start(f32[248,128]{1,0:T(8,128)S(1)} %get-tuple-element.18), channel_id=1, source_target_pairs={{1,2},{2,1},{3,4},{4,3},{5,6},{6,5},{9,10},{10,9},{11,12},{12,11},... | collective-permute-start | bytes 380936 | tf_op jit(solution)/shard_map/ppermute | solution.py:370
  32.7 3.2 %collective-permute-start.4 = (f32[248,128]{1,0:T(8,128)S(1)}, f32[248,128]{1,0:T(8,128)S(1)}, u32[]{:S(2)}, u32[]{:S(2)}) collective-permute-start(f32[248,128]{1,0:T(8,128)S(1)} %get-tuple-element.19), channel_id=1, source_target_pairs={{0,1},{1,0},{2,3},{3,2},{4,5},{5,4},{6,7},{7,6},{8,9},{9,8},{10,11... | collective-permute-start | bytes 380936 | tf_op jit(solution)/shard_map/ppermute | solution.py:370

commit v5 on v4

--- a/solution.py
+++ b/solution.py
@@ -51,7 +51,7 @@
     return old, nxt, new
 
 
-def pre_kernel(uc, pc, mc, muc, lamc, rhoc, qc, omc, uf, pf, mf, muf, lamf, rhof, qf, omf, st, out1, out2, out3, own_f, own_c):
+def pre_kernel(uc, pc, mc, muc, lamc, rhoc, qc, omc, uf, pf, mf, muf, lamf, rhof, qf, omf, st, out1, out2, own_f, own_c):
     even = lax.rem(lax.axis_index("gx"), 2) == 0
     outer_first = far_first(lax.axis_index("gy"))
     eye = lax.broadcasted_iota(jnp.int32, (8, 8), 0) == lax.broadcasted_iota(jnp.int32, (8, 8), 1)
@@ -105,21 +105,23 @@
             def _(is_even=is_even, is_first=is_first):
                 message(out1 if is_first else out2, not is_even)
                 message(out2 if is_first else out1, is_even)
-                message(out3, not is_even)
-
-
-def mid_kernel(own_f, own_c, r1, r2, r3, out2, out1, halo):
+
+
+def mid_kernel(own_f, own_c, r1, r2, out2, out1, halo):
     gx, gy = lax.axis_index("gx"), lax.axis_index("gy")
     even_x = lax.rem(gx, 2) == 0
     even_y = lax.rem(gy, 2) == 0
-    inner_at = jnp.where(far_first(gy), 1, 0)
-    outer_at = jnp.where(late(gx), 2, 1 - inner_at)
-    for side, at in ((0, jnp.where(even_x, outer_at, inner_at)), (1, jnp.where(even_x, inner_at, outer_at))):
-        for k, r in enumerate((r1, r2, r3)):
-
-            @pl.when(at == k)
-            def _(side=side, r=r):
-                halo[side] = r[...]
+    left_first = even_x == far_first(gy)
+
+    @pl.when(left_first)
+    def _():
+        halo[0] = r1[...]
+        halo[1] = r2[...]
+
+    @pl.when(jnp.logical_not(left_first))
+    def _():
+        halo[0] = r2[...]
+        halo[1] = r1[...]
 
     def message(out, up):
         for key, (at, rows) in Y_AT.items():
@@ -336,31 +338,18 @@
 SCRATCH = 3 * (10 + 6 + 6 + 4)
 
 
-X_RUN, SEAM = 4, 12
-
-
-def late(gx):
-    at = gx % SEAM
-    if isinstance(gx, int):
-        return at == SEAM - 1 or (at != 0 and at % X_RUN == 0)
-    return jnp.logical_or(at == SEAM - 1, jnp.logical_and(at != 0, lax.rem(at, X_RUN) == 0))
-
-
 def far_first(gy):
     return gy < -(-5 * lax.axis_size("gy") // 8)
 
 
-def x_exchange(first, second, third):
+def x_exchange(first, second):
     nx, ny = lax.axis_size("gx"), lax.axis_size("gy")
-    pairs = [[], [], []]
+    pairs = [[], []]
     for i in range(nx - 1):
         for j in range(ny):
-            outer = i % 2 == 1
-            turn = 0 if outer == far_first(j) else 1
-            for source, target in ((i, i + 1), (i + 1, i)):
-                held = outer and i % X_RUN == X_RUN - 1 and late(target)
-                pairs[2 if held else turn].append((source * ny + j, target * ny + j))
-    return [lax.ppermute(v, ("gx", "gy"), p) for v, p in zip((first, second, third), pairs)]
+            turn = 0 if (i % 2 == 1) == far_first(j) else 1
+            pairs[turn] += [(i * ny + j, (i + 1) * ny + j), ((i + 1) * ny + j, i * ny + j)]
+    return [lax.ppermute(v, ("gx", "gy"), p) for v, p in zip((first, second), pairs)]
 
 
 def swap(value, axis, first):
@@ -406,14 +395,14 @@
     omega_f,
     stretch_f,
 ):
-    out1, out2, out3, own_f, own_c = call(
-        pre_kernel, [(X_ROWS, LANES)] * 3 + [(36, 8, LANES), (16, 4, LANES)], first=True
+    out1, out2, own_f, own_c = call(
+        pre_kernel, [(X_ROWS, LANES)] * 2 + [(36, 8, LANES), (16, 4, LANES)], first=True
     )(
         u_now_c, u_prev_c, memory_c, mu_c, lam_c, rho_c, q_c, omega_c,
         u_now_f, u_prev_f, memory_f, mu_f, lam_f, rho_f, q_f, omega_f, stretch_f,
     )
     out2, out1, halo = call(mid_kernel, [(Y_ROWS, LANES)] * 2 + [(2, X_ROWS, LANES)])(
-        own_f, own_c, *x_exchange(out1, out2, out3)
+        own_f, own_c, *x_exchange(out1, out2)
     )
     y2 = swap(out2, "gy", 1)
     y1 = swap(out1, "gy", 0)

time: 37.6 us -> 34.6 us (0.920)
  starting transfers between devices: 31.1 us -> 26.3 us
  waiting for transfers between devices: 2.68 us -> 4.47 us
    ppermute x3 -> x2, starting transfers between devices: 21.9 us -> 19.2 us  [x_exchange(): lax.ppermute(v, ('gx', 'gy'), p)]
    ppermute x2, starting transfers between devices: 9.18 us -> 7.14 us  [swap(): return lax.ppermute(value, axis, pairs)]
    ppermute x3 -> x2, waiting for transfers between devices: 1.37 us -> 3.16 us  [x_exchange(): lax.ppermute(v, ('gx', 'gy'), p)]
  transfers between devices with their start and end apart: 5 -> 4, of which waited for: 3 -> 3; matrix products, arithmetic and copies ran while one was open for 0% -> 0% of each run, Pallas kernels for 0% -> 0%
where the time goes in v5:
time: 34.6 us; the launch traced here: 34.3 us
  starting transfers between devices  26.3 us (76%)
  waiting for transfers between devices  4.47 us (13%)
  Pallas kernels  2.74 us (8%)
  between operations  0.77 us (2%)
    ppermute x2, starting transfers between devices, x_exchange(): lax.ppermute(v, ('gx', 'gy'), p)  19.2 us
    ppermute x2, starting transfers between devices, swap(): return lax.ppermute(value, axis, pairs)  7.14 us
    ppermute x2, waiting for transfers between devices, x_exchange(): lax.ppermute(v, ('gx', 'gy'), p)  3.16 us
    pallas_call x3, Pallas kernels, run(): pl.pallas_call(kernel, out_shape=[(jax.ShapeDtypeStruct if last else pltp...  2.74 us
    ppermute x2, waiting for transfers between devices, swap(): return lax.ppermute(value, axis, pairs)  1.31 us
  transfers between devices with their start and end apart: 4, of which 3 were waited for; matrix products, arithmetic and copies ran while one was open for 0% of the time, Pallas kernels for 0%

profile of v5, /device:TPU:57, one launch (start us, length us, event | category | flops | bytes accessed | tf_op | source)
XLA Modules:
  0.0 34.3 jit_solution(3492130671813230136)
XLA Ops:
  0.6 0.0 copy-start.5
  0.6 0.0 copy-start.6
  0.7 0.0 copy-start.7
  0.7 1.3 %shard_map.192 = (f32[144,128]{1,0:T(8,128)S(1)}, f32[144,128]{1,0:T(8,128)S(1)}, f32[36,8,128]{2,1,0:T(8,128)S(1)}, f32[16,4,128]{2,1,0:T(4,128)S(1)}) custom-call(f32[3,2,4,128]{3,2,1,0:T(4,128)} %uc.3, f32[3,2,4,128]{3,2,1,0:T(4,128)} %pc.1, f32[3,3,2,4,128]{4,3,2,1,0:T(4,128)} %mc.3, f32[2,4,128]{2,1,0:T(4,128)} %muc.1, f32[2,4,128]{2,1,0:T(4,128)} %lamc.1, ...), custom_call_target="tpu_custom_call" | custom-call | tf_op jit(solution)/shard_map/pallas_call | solution.py:368
  2.0 17.3 %collective-permute-start = (f32[144,128]{1,0:T(8,128)S(1)}, f32[144,128]{1,0:T(8,128)S(1)}, u32[]{:S(2)}, u32[]{:S(2)}) collective-permute-start(f32[144,128]{1,0:T(8,128)S(1)} %get-tuple-element.13), channel_id=1, source_target_pairs={{5,13},{13,5},{6,14},{14,6},{7,15},{15,7},{8,16},{16,8},{9,17},{17... | collective-permute-start | bytes 221192 | tf_op jit(solution)/shard_map/ppermute | solution.py:352
  19.2 1.9 %collective-permute-start.1 = (f32[144,128]{1,0:T(8,128)S(1)}, f32[144,128]{1,0:T(8,128)S(1)}, u32[]{:S(2)}, u32[]{:S(2)}) collective-permute-start(f32[144,128]{1,0:T(8,128)S(1)} %get-tuple-element.14), channel_id=1, source_target_pairs={{0,8},{8,0},{1,9},{9,1},{2,10},{10,2},{3,11},{11,3},{4,12},{12,4},... | collective-permute-start | bytes 221192 | tf_op jit(solution)/shard_map/ppermute | solution.py:352
  21.2 0.0 collective-permute-done.r1
  21.2 3.2 %collective-permute-done.1.r2 = f32[144,128]{1,0:T(8,128)S(1)} collective-permute-done((f32[144,128]{1,0:T(8,128)S(1)}, f32[144,128]{1,0:T(8,128)S(1)}, u32[]{:S(2)}, u32[]{:S(2)}) %collective-permute-start.1) | collective-permute-done | bytes 73760 | tf_op jit(solution)/shard_map/ppermute | solution.py:352
  24.3 0.0 copy-start
  24.3 0.0 copy-start.1
  24.3 0.0 copy-start.2
  24.4 0.0 copy-start.3
  24.4 0.0 copy-start.4
  24.4 0.1 shard_map.193
  24.5 5.2 %collective-permute-start.2 = (f32[248,128]{1,0:T(8,128)S(1)}, f32[248,128]{1,0:T(8,128)S(1)}, u32[]{:S(2)}, u32[]{:S(2)}) collective-permute-start(f32[248,128]{1,0:T(8,128)S(1)} %get-tuple-element.16), channel_id=1, source_target_pairs={{1,2},{2,1},{3,4},{4,3},{5,6},{6,5},{9,10},{10,9},{11,12},{12,11},... | collective-permute-start | bytes 380936 | tf_op jit(solution)/shard_map/ppermute | solution.py:359
  29.7 1.9 %collective-permute-start.3 = (f32[248,128]{1,0:T(8,128)S(1)}, f32[248,128]{1,0:T(8,128)S(1)}, u32[]{:S(2)}, u32[]{:S(2)}) collective-permute-start(f32[248,128]{1,0:T(8,128)S(1)} %get-tuple-element.17), channel_id=1, source_target_pairs={{0,1},{1,0},{2,3},{3,2},{4,5},{5,4},{6,7},{7,6},{8,9},{9,8},{10,11... | collective-permute-start | bytes 380936 | tf_op jit(solution)/shard_map/ppermute | solution.py:359
  31.6 0.7 %collective-permute-done.2.y2 = f32[248,128]{1,0:T(8,128)S(1)} collective-permute-done((f32[248,128]{1,0:T(8,128)S(1)}, f32[248,128]{1,0:T(8,128)S(1)}, u32[]{:S(2)}, u32[]{:S(2)}) %collective-permute-start.2) | collective-permute-done | bytes 127008 | tf_op jit(solution)/shard_map/ppermute | solution.py:359
  32.3 0.6 %collective-permute-done.3.y1 = f32[248,128]{1,0:T(8,128)S(1)} collective-permute-done((f32[248,128]{1,0:T(8,128)S(1)}, f32[248,128]{1,0:T(8,128)S(1)}, u32[]{:S(2)}, u32[]{:S(2)}) %collective-permute-start.3) | collective-permute-done | bytes 127008 | tf_op jit(solution)/shard_map/ppermute | solution.py:359
  33.0 0.0 copy-done.5
  33.0 0.0 copy-done.6
  33.0 0.0 copy-done.7
  33.0 0.0 copy-done
  33.0 0.0 copy-done.1
  33.0 0.0 copy-done.2
  33.0 0.0 copy-done.3
  33.0 0.0 copy-done.4
  33.0 1.3 %shard_map.194 = (f32[3,2,4,128]{3,2,1,0:T(4,128)}, f32[3,4,8,128]{3,2,1,0:T(8,128)}, f32[3,3,2,4,128]{4,3,2,1,0:T(4,128)}, f32[3,3,4,8,128]{4,3,2,1,0:T(8,128)}) custom-call(f32[36,8,128]{2,1,0:T(8,128)S(1)} %get-tuple-element.11.own_f, f32[16,4,128]{2,1,0:T(4,128)S(1)} %get-tuple-element.12.own_c, f32[2,144,128]{2,1,0:T(8,128)S(1)} %get-tuple-element.15.hx, ...), custom_call_target="tpu_custom_call" | custom-call | tf_op jit(solution)/shard_map/pallas_call | solution.py:368
Async XLA Ops:
  0.6 32.3 %copy-start.5 = (f32[3,2,4,128]{3,2,1,0:T(4,128)S(1)}, f32[3,2,4,128]{3,2,1,0:T(4,128)}, u32[]{:S(2)}) copy-start(f32[3,2,4,128]{3,2,1,0:T(4,128)} %uc.3) | copy-start | bytes 36868
  0.6 32.3 %copy-start.6 = (f32[3,2,4,128]{3,2,1,0:T(4,128)S(1)}, f32[3,2,4,128]{3,2,1,0:T(4,128)}, u32[]{:S(2)}) copy-start(f32[3,2,4,128]{3,2,1,0:T(4,128)} %qc.3) | copy-start | bytes 36868
  0.7 32.3 %copy-start.7 = (f32[3,2,4,128]{3,2,1,0:T(4,128)S(1)}, f32[3,2,4,128]{3,2,1,0:T(4,128)}, u32[]{:S(2)}) copy-start(f32[3,2,4,128]{3,2,1,0:T(4,128)} %omc.3) | copy-start | bytes 36868
  2.0 19.2 %collective-permute-start = (f32[144,128]{1,0:T(8,128)S(1)}, f32[144,128]{1,0:T(8,128)S(1)}, u32[]{:S(2)}, u32[]{:S(2)}) collective-permute-start(f32[144,128]{1,0:T(8,128)S(1)} %get-tuple-element.13), channel_id=1, source_target_pairs={{5,13},{13,5},{6,14},{14,6},{7,15},{15,7},{8,16},{16,8},{9,17},{17... | collective-permute-start | bytes 221192 | tf_op jit(solution)/shard_map/ppermute | solution.py:352
  19.2 5.1 %collective-permute-start.1 = (f32[144,128]{1,0:T(8,128)S(1)}, f32[144,128]{1,0:T(8,128)S(1)}, u32[]{:S(2)}, u32[]{:S(2)}) collective-permute-start(f32[144,128]{1,0:T(8,128)S(1)} %get-tuple-element.14), channel_id=1, source_target_pairs={{0,8},{8,0},{1,9},{9,1},{2,10},{10,2},{3,11},{11,3},{4,12},{12,4},... | collective-permute-start | bytes 221192 | tf_op jit(solution)/shard_map/ppermute | solution.py:352
  24.3 8.6 %copy-start = (f32[3,3,4,8,128]{4,3,2,1,0:T(8,128)S(1)}, f32[3,3,4,8,128]{4,3,2,1,0:T(8,128)}, u32[]{:S(2)}) copy-start(f32[3,3,4,8,128]{4,3,2,1,0:T(8,128)} %mf.3) | copy-start | bytes 442372
  24.3 8.6 %copy-start.1 = (f32[3,4,8,128]{3,2,1,0:T(8,128)S(1)}, f32[3,4,8,128]{3,2,1,0:T(8,128)}, u32[]{:S(2)}) copy-start(f32[3,4,8,128]{3,2,1,0:T(8,128)} %uf.3) | copy-start | bytes 147460
  24.3 8.6 %copy-start.2 = (f32[3,4,8,128]{3,2,1,0:T(8,128)S(1)}, f32[3,4,8,128]{3,2,1,0:T(8,128)}, u32[]{:S(2)}) copy-start(f32[3,4,8,128]{3,2,1,0:T(8,128)} %qf.3) | copy-start | bytes 147460
  24.4 8.6 %copy-start.3 = (f32[3,4,8,128]{3,2,1,0:T(8,128)S(1)}, f32[3,4,8,128]{3,2,1,0:T(8,128)}, u32[]{:S(2)}) copy-start(f32[3,4,8,128]{3,2,1,0:T(8,128)} %omf.3) | copy-start | bytes 147460
  24.4 8.7 %copy-start.4 = (f32[3,3,2,4,128]{4,3,2,1,0:T(4,128)S(1)}, f32[3,3,2,4,128]{4,3,2,1,0:T(4,128)}, u32[]{:S(2)}) copy-start(f32[3,3,2,4,128]{4,3,2,1,0:T(4,128)} %mc.3) | copy-start | bytes 110596
  24.5 7.8 %collective-permute-start.2 = (f32[248,128]{1,0:T(8,128)S(1)}, f32[248,128]{1,0:T(8,128)S(1)}, u32[]{:S(2)}, u32[]{:S(2)}) collective-permute-start(f32[248,128]{1,0:T(8,128)S(1)} %get-tuple-element.16), channel_id=1, source_target_pairs={{1,2},{2,1},{3,4},{4,3},{5,6},{6,5},{9,10},{10,9},{11,12},{12,11},... | collective-permute-start | bytes 380936 | tf_op jit(solution)/shard_map/ppermute | solution.py:359
  29.7 3.2 %collective-permute-start.3 = (f32[248,128]{1,0:T(8,128)S(1)}, f32[248,128]{1,0:T(8,128)S(1)}, u32[]{:S(2)}, u32[]{:S(2)}) collective-permute-start(f32[248,128]{1,0:T(8,128)S(1)} %get-tuple-element.17), channel_id=1, source_target_pairs={{0,1},{1,0},{2,3},{3,2},{4,5},{5,4},{6,7},{7,6},{8,9},{9,8},{10,11... | collective-permute-start | bytes 380936 | tf_op jit(solution)/shard_map/ppermute | solution.py:359

commit v6 on v4

--- a/solution.py
+++ b/solution.py
@@ -52,8 +52,9 @@
 
 
 def pre_kernel(uc, pc, mc, muc, lamc, rhoc, qc, omc, uf, pf, mf, muf, lamf, rhof, qf, omf, st, out1, out2, out3, own_f, own_c):
-    even = lax.rem(lax.axis_index("gx"), 2) == 0
-    outer_first = far_first(lax.axis_index("gy"))
+    gx = lax.axis_index("gx")
+    even = lax.rem(gx, 2) == 0
+    outer_turn, inner_turn = x_turns(gx, lax.axis_index("gy"))
     eye = lax.broadcasted_iota(jnp.int32, (8, 8), 0) == lax.broadcasted_iota(jnp.int32, (8, 8), 1)
     lane = lax.broadcasted_iota(jnp.int32, (8, LANES), 1)
 
@@ -98,28 +99,35 @@
         at = X_AT["bits"][0]
         out[at : at + 8] = bits
 
-    for is_even in (True, False):
-        for is_first in (True, False):
-
-            @pl.when(jnp.logical_and(even == is_even, outer_first == is_first))
-            def _(is_even=is_even, is_first=is_first):
-                message(out1 if is_first else out2, not is_even)
-                message(out2 if is_first else out1, is_even)
-                message(out3, not is_even)
+    for turn, out in enumerate((out1, out2, out3)):
+        go_left = jnp.where(even, outer_turn, inner_turn) == turn
+        go_right = jnp.where(even, inner_turn, outer_turn) == turn
+
+        @pl.when(go_left)
+        def _(out=out):
+            message(out, False)
+
+        @pl.when(go_right)
+        def _(out=out):
+            message(out, True)
 
 
 def mid_kernel(own_f, own_c, r1, r2, r3, out2, out1, halo):
     gx, gy = lax.axis_index("gx"), lax.axis_index("gy")
     even_x = lax.rem(gx, 2) == 0
     even_y = lax.rem(gy, 2) == 0
-    inner_at = jnp.where(far_first(gy), 1, 0)
-    outer_at = jnp.where(late(gx), 2, 1 - inner_at)
-    for side, at in ((0, jnp.where(even_x, outer_at, inner_at)), (1, jnp.where(even_x, inner_at, outer_at))):
-        for k, r in enumerate((r1, r2, r3)):
-
-            @pl.when(at == k)
-            def _(side=side, r=r):
-                halo[side] = r[...]
+    outer_turn, inner_turn = x_turns(gx, gy)
+    for turn, r in enumerate((r1, r2, r3)):
+        from_left = jnp.where(even_x, outer_turn, inner_turn) == turn
+        from_right = jnp.where(even_x, inner_turn, outer_turn) == turn
+
+        @pl.when(from_left)
+        def _(r=r):
+            halo[0] = r[...]
+
+        @pl.when(from_right)
+        def _(r=r):
+            halo[1] = r[...]
 
     def message(out, up):
         for key, (at, rows) in Y_AT.items():
@@ -339,28 +347,23 @@
 X_RUN, SEAM = 4, 12
 
 
-def late(gx):
+def x_turns(gx, gy):
     at = gx % SEAM
+    early = (at == 0) | (at == 1) | (at == 2) | (at == 3) | (at == 6) | (at == 7)
+    soon = gy < -(-5 * lax.axis_size("gy") // 8)
     if isinstance(gx, int):
-        return at == SEAM - 1 or (at != 0 and at % X_RUN == 0)
-    return jnp.logical_or(at == SEAM - 1, jnp.logical_and(at != 0, lax.rem(at, X_RUN) == 0))
-
-
-def far_first(gy):
-    return gy < -(-5 * lax.axis_size("gy") // 8)
-
-
-def x_exchange(first, second, third):
+        return (1 if soon else 2), (0 if early else 2 if soon else 1)
+    return jnp.where(soon, 1, 2), jnp.where(early, 0, jnp.where(soon, 2, 1))
+
+
+def x_exchange(messages):
     nx, ny = lax.axis_size("gx"), lax.axis_size("gy")
     pairs = [[], [], []]
     for i in range(nx - 1):
         for j in range(ny):
-            outer = i % 2 == 1
-            turn = 0 if outer == far_first(j) else 1
-            for source, target in ((i, i + 1), (i + 1, i)):
-                held = outer and i % X_RUN == X_RUN - 1 and late(target)
-                pairs[2 if held else turn].append((source * ny + j, target * ny + j))
-    return [lax.ppermute(v, ("gx", "gy"), p) for v, p in zip((first, second, third), pairs)]
+            turn = x_turns(i, j)[0 if i % 2 == 1 else 1]
+            pairs[turn] += [(i * ny + j, (i + 1) * ny + j), ((i + 1) * ny + j, i * ny + j)]
+    return [lax.ppermute(v, ("gx", "gy"), p) for v, p in zip(messages, pairs)]
 
 
 def swap(value, axis, first):
@@ -413,7 +416,7 @@
         u_now_f, u_prev_f, memory_f, mu_f, lam_f, rho_f, q_f, omega_f, stretch_f,
     )
     out2, out1, halo = call(mid_kernel, [(Y_ROWS, LANES)] * 2 + [(2, X_ROWS, LANES)])(
-        own_f, own_c, *x_exchange(out1, out2, out3)
+        own_f, own_c, *x_exchange((out1, out2, out3))
     )
     y2 = swap(out2, "gy", 1)
     y1 = swap(out1, "gy", 0)

time: 37.6 us -> 34.3 us (0.912)
  the two profiles are of different devices: /device:TPU:57 before, /device:TPU:177 now
where the time goes in v6:
time: 34.3 us; the launch traced here: 34 us
  starting transfers between devices  25.6 us (75%)
  waiting for transfers between devices  4.72 us (14%)
  Pallas kernels  2.84 us (8%)
  between operations  0.79 us (2%)
    ppermute x3, starting transfers between devices, x_exchange(): return [lax.ppermute(v, ('gx', 'gy'), p) for v, p in zip(messages, pairs)]  18.6 us
    ppermute x2, starting transfers between devices, swap(): return lax.ppermute(value, axis, pairs)  7.06 us
    ppermute x3, waiting for transfers between devices, x_exchange(): return [lax.ppermute(v, ('gx', 'gy'), p) for v, p in zip(messages, pairs)]  3.42 us
    pallas_call x3, Pallas kernels, run(): pl.pallas_call(kernel, out_shape=[(jax.ShapeDtypeStruct if last else pltp...  2.84 us
    ppermute x2, waiting for transfers between devices, swap(): return lax.ppermute(value, axis, pairs)  1.31 us
  transfers between devices with their start and end apart: 5, of which 3 were waited for; matrix products, arithmetic and copies ran while one was open for 0% of the time, Pallas kernels for 0%

profile of v6, /device:TPU:177, one launch (start us, length us, event | category | flops | bytes accessed | tf_op | source)
XLA Modules:
  0.0 34.0 jit_solution(10375531116141637537)
XLA Ops:
  0.6 1.4 %shard_map.192 = (f32[144,128]{1,0:T(8,128)S(1)}, f32[144,128]{1,0:T(8,128)S(1)}, f32[144,128]{1,0:T(8,128)S(1)}, f32[36,8,128]{2,1,0:T(8,128)S(1)}, f32[16,4,128]{2,1,0:T(4,128)S(1)}) custom-call(f32[3,2,4,128]{3,2,1,0:T(4,128)} %uc.3, f32[3,2,4,128]{3,2,1,0:T(4,128)} %pc.1, f32[3,3,2,4,128]{4,3,2,1,0:T(4,128)} %mc.3, f32[2,4,128]{2,1,0:T(4,128)} %muc.1, ...), custom_call_target="tpu_custom_call" | custom-call | tf_op jit(solution)/shard_map/pallas_call | solution.py:382
  2.0 3.1 %collective-permute-start = (f32[144,128]{1,0:T(8,128)S(1)}, f32[144,128]{1,0:T(8,128)S(1)}, u32[]{:S(2)}, u32[]{:S(2)}) collective-permute-start(f32[144,128]{1,0:T(8,128)S(1)} %get-tuple-element.14), channel_id=1, source_target_pairs={{0,8},{8,0},{1,9},{9,1},{2,10},{10,2},{3,11},{11,3},{4,12},{12,4},... | collective-permute-start | bytes 221192 | tf_op jit(solution)/shard_map/ppermute | solution.py:366
  5.1 0.7 %collective-permute-start.1 = (f32[144,128]{1,0:T(8,128)S(1)}, f32[144,128]{1,0:T(8,128)S(1)}, u32[]{:S(2)}, u32[]{:S(2)}) collective-permute-start(f32[144,128]{1,0:T(8,128)S(1)} %get-tuple-element.15), channel_id=1, source_target_pairs={{8,16},{16,8},{9,17},{17,9},{10,18},{18,10},{11,19},{19,11},{12,20... | collective-permute-start | bytes 221192 | tf_op jit(solution)/shard_map/ppermute | solution.py:366
  5.8 14.8 %collective-permute-start.2 = (f32[144,128]{1,0:T(8,128)S(1)}, f32[144,128]{1,0:T(8,128)S(1)}, u32[]{:S(2)}, u32[]{:S(2)}) collective-permute-start(f32[144,128]{1,0:T(8,128)S(1)} %get-tuple-element.16), channel_id=1, source_target_pairs={{13,21},{21,13},{14,22},{22,14},{15,23},{23,15},{29,37},{37,29},{3... | collective-permute-start | bytes 221192 | tf_op jit(solution)/shard_map/ppermute | solution.py:366
  20.6 0.0 collective-permute-done.r1
  20.6 0.0 collective-permute-done.1.r2
  20.6 3.4 %collective-permute-done.2.r3 = f32[144,128]{1,0:T(8,128)S(1)} collective-permute-done((f32[144,128]{1,0:T(8,128)S(1)}, f32[144,128]{1,0:T(8,128)S(1)}, u32[]{:S(2)}, u32[]{:S(2)}) %collective-permute-start.2) | collective-permute-done | bytes 73760 | tf_op jit(solution)/shard_map/ppermute | solution.py:366
  24.1 0.0 copy-start
  24.1 0.0 copy-start.1
  24.1 0.0 copy-start.2
  24.1 0.0 copy-start.3
  24.1 0.0 copy-start.4
  24.1 0.0 copy-start.5
  24.1 0.0 copy-start.6
  24.1 0.0 copy-start.7
  24.1 0.1 shard_map.193
  24.3 5.1 %collective-permute-start.3 = (f32[248,128]{1,0:T(8,128)S(1)}, f32[248,128]{1,0:T(8,128)S(1)}, u32[]{:S(2)}, u32[]{:S(2)}) collective-permute-start(f32[248,128]{1,0:T(8,128)S(1)} %get-tuple-element.18), channel_id=1, source_target_pairs={{1,2},{2,1},{3,4},{4,3},{5,6},{6,5},{9,10},{10,9},{11,12},{12,11},... | collective-permute-start | bytes 380936 | tf_op jit(solution)/shard_map/ppermute | solution.py:373
  29.4 1.9 %collective-permute-start.4 = (f32[248,128]{1,0:T(8,128)S(1)}, f32[248,128]{1,0:T(8,128)S(1)}, u32[]{:S(2)}, u32[]{:S(2)}) collective-permute-start(f32[248,128]{1,0:T(8,128)S(1)} %get-tuple-element.19), channel_id=1, source_target_pairs={{0,1},{1,0},{2,3},{3,2},{4,5},{5,4},{6,7},{7,6},{8,9},{9,8},{10,11... | collective-permute-start | bytes 380936 | tf_op jit(solution)/shard_map/ppermute | solution.py:373
  31.3 0.7 %collective-permute-done.3.y2 = f32[248,128]{1,0:T(8,128)S(1)} collective-permute-done((f32[248,128]{1,0:T(8,128)S(1)}, f32[248,128]{1,0:T(8,128)S(1)}, u32[]{:S(2)}, u32[]{:S(2)}) %collective-permute-start.3) | collective-permute-done | bytes 127008 | tf_op jit(solution)/shard_map/ppermute | solution.py:373
  32.0 0.6 %collective-permute-done.4.y1 = f32[248,128]{1,0:T(8,128)S(1)} collective-permute-done((f32[248,128]{1,0:T(8,128)S(1)}, f32[248,128]{1,0:T(8,128)S(1)}, u32[]{:S(2)}, u32[]{:S(2)}) %collective-permute-start.4) | collective-permute-done | bytes 127008 | tf_op jit(solution)/shard_map/ppermute | solution.py:373
  32.6 0.0 copy-done
  32.6 0.0 copy-done.1
  32.7 0.0 copy-done.2
  32.7 0.0 copy-done.3
  32.7 0.0 copy-done.4
  32.7 0.0 copy-done.5
  32.7 0.0 copy-done.6
  32.7 0.0 copy-done.7
  32.7 1.3 %shard_map.194 = (f32[3,2,4,128]{3,2,1,0:T(4,128)}, f32[3,4,8,128]{3,2,1,0:T(8,128)}, f32[3,3,2,4,128]{4,3,2,1,0:T(4,128)}, f32[3,3,4,8,128]{4,3,2,1,0:T(8,128)}) custom-call(f32[36,8,128]{2,1,0:T(8,128)S(1)} %get-tuple-element.12.own_f, f32[16,4,128]{2,1,0:T(4,128)S(1)} %get-tuple-element.13.own_c, f32[2,144,128]{2,1,0:T(8,128)S(1)} %get-tuple-element.17.hx, ...), custom_call_target="tpu_custom_call" | custom-call | tf_op jit(solution)/shard_map/pallas_call | solution.py:382
Async XLA Ops:
  2.0 18.6 %collective-permute-start = (f32[144,128]{1,0:T(8,128)S(1)}, f32[144,128]{1,0:T(8,128)S(1)}, u32[]{:S(2)}, u32[]{:S(2)}) collective-permute-start(f32[144,128]{1,0:T(8,128)S(1)} %get-tuple-element.14), channel_id=1, source_target_pairs={{0,8},{8,0},{1,9},{9,1},{2,10},{10,2},{3,11},{11,3},{4,12},{12,4},... | collective-permute-start | bytes 221192 | tf_op jit(solution)/shard_map/ppermute | solution.py:366
  5.1 15.5 %collective-permute-start.1 = (f32[144,128]{1,0:T(8,128)S(1)}, f32[144,128]{1,0:T(8,128)S(1)}, u32[]{:S(2)}, u32[]{:S(2)}) collective-permute-start(f32[144,128]{1,0:T(8,128)S(1)} %get-tuple-element.15), channel_id=1, source_target_pairs={{8,16},{16,8},{9,17},{17,9},{10,18},{18,10},{11,19},{19,11},{12,20... | collective-permute-start | bytes 221192 | tf_op jit(solution)/shard_map/ppermute | solution.py:366
  5.8 18.3 %collective-permute-start.2 = (f32[144,128]{1,0:T(8,128)S(1)}, f32[144,128]{1,0:T(8,128)S(1)}, u32[]{:S(2)}, u32[]{:S(2)}) collective-permute-start(f32[144,128]{1,0:T(8,128)S(1)} %get-tuple-element.16), channel_id=1, source_target_pairs={{13,21},{21,13},{14,22},{22,14},{15,23},{23,15},{29,37},{37,29},{3... | collective-permute-start | bytes 221192 | tf_op jit(solution)/shard_map/ppermute | solution.py:366
  24.1 8.6 %copy-start = (f32[3,3,4,8,128]{4,3,2,1,0:T(8,128)S(1)}, f32[3,3,4,8,128]{4,3,2,1,0:T(8,128)}, u32[]{:S(2)}) copy-start(f32[3,3,4,8,128]{4,3,2,1,0:T(8,128)} %mf.3) | copy-start | bytes 442372
  24.1 8.6 %copy-start.1 = (f32[3,4,8,128]{3,2,1,0:T(8,128)S(1)}, f32[3,4,8,128]{3,2,1,0:T(8,128)}, u32[]{:S(2)}) copy-start(f32[3,4,8,128]{3,2,1,0:T(8,128)} %uf.3) | copy-start | bytes 147460
  24.1 8.6 %copy-start.2 = (f32[3,4,8,128]{3,2,1,0:T(8,128)S(1)}, f32[3,4,8,128]{3,2,1,0:T(8,128)}, u32[]{:S(2)}) copy-start(f32[3,4,8,128]{3,2,1,0:T(8,128)} %qf.3) | copy-start | bytes 147460
  24.1 8.6 %copy-start.3 = (f32[3,4,8,128]{3,2,1,0:T(8,128)S(1)}, f32[3,4,8,128]{3,2,1,0:T(8,128)}, u32[]{:S(2)}) copy-start(f32[3,4,8,128]{3,2,1,0:T(8,128)} %omf.3) | copy-start | bytes 147460
  24.1 8.6 %copy-start.4 = (f32[3,3,2,4,128]{4,3,2,1,0:T(4,128)S(1)}, f32[3,3,2,4,128]{4,3,2,1,0:T(4,128)}, u32[]{:S(2)}) copy-start(f32[3,3,2,4,128]{4,3,2,1,0:T(4,128)} %mc.3) | copy-start | bytes 110596
  24.1 8.6 %copy-start.5 = (f32[3,2,4,128]{3,2,1,0:T(4,128)S(1)}, f32[3,2,4,128]{3,2,1,0:T(4,128)}, u32[]{:S(2)}) copy-start(f32[3,2,4,128]{3,2,1,0:T(4,128)} %uc.3) | copy-start | bytes 36868
  24.1 8.6 %copy-start.6 = (f32[3,2,4,128]{3,2,1,0:T(4,128)S(1)}, f32[3,2,4,128]{3,2,1,0:T(4,128)}, u32[]{:S(2)}) copy-start(f32[3,2,4,128]{3,2,1,0:T(4,128)} %qc.3) | copy-start | bytes 36868
  24.1 8.6 %copy-start.7 = (f32[3,2,4,128]{3,2,1,0:T(4,128)S(1)}, f32[3,2,4,128]{3,2,1,0:T(4,128)}, u32[]{:S(2)}) copy-start(f32[3,2,4,128]{3,2,1,0:T(4,128)} %omc.3) | copy-start | bytes 36868
  24.3 7.7 %collective-permute-start.3 = (f32[248,128]{1,0:T(8,128)S(1)}, f32[248,128]{1,0:T(8,128)S(1)}, u32[]{:S(2)}, u32[]{:S(2)}) collective-permute-start(f32[248,128]{1,0:T(8,128)S(1)} %get-tuple-element.18), channel_id=1, source_target_pairs={{1,2},{2,1},{3,4},{4,3},{5,6},{6,5},{9,10},{10,9},{11,12},{12,11},... | collective-permute-start | bytes 380936 | tf_op jit(solution)/shard_map/ppermute | solution.py:373
  29.4 3.2 %collective-permute-start.4 = (f32[248,128]{1,0:T(8,128)S(1)}, f32[248,128]{1,0:T(8,128)S(1)}, u32[]{:S(2)}, u32[]{:S(2)}) collective-permute-start(f32[248,128]{1,0:T(8,128)S(1)} %get-tuple-element.19), channel_id=1, source_target_pairs={{0,1},{1,0},{2,3},{3,2},{4,5},{5,4},{6,7},{7,6},{8,9},{9,8},{10,11... | collective-permute-start | bytes 380936 | tf_op jit(solution)/shard_map/ppermute | solution.py:373

commit v7 on v5

--- a/solution.py
+++ b/solution.py
@@ -51,9 +51,8 @@
     return old, nxt, new
 
 
-def pre_kernel(uc, pc, mc, muc, lamc, rhoc, qc, omc, uf, pf, mf, muf, lamf, rhof, qf, omf, st, out1, out2, own_f, own_c):
+def pre_kernel(uc, pc, mc, muc, lamc, rhoc, qc, omc, uf, pf, mf, muf, lamf, rhof, qf, omf, st, inner, outer, own_f, own_c):
     even = lax.rem(lax.axis_index("gx"), 2) == 0
-    outer_first = far_first(lax.axis_index("gy"))
     eye = lax.broadcasted_iota(jnp.int32, (8, 8), 0) == lax.broadcasted_iota(jnp.int32, (8, 8), 1)
     lane = lax.broadcasted_iota(jnp.int32, (8, LANES), 1)
 
@@ -98,30 +97,44 @@
         at = X_AT["bits"][0]
         out[at : at + 8] = bits
 
-    for is_even in (True, False):
-        for is_first in (True, False):
-
-            @pl.when(jnp.logical_and(even == is_even, outer_first == is_first))
-            def _(is_even=is_even, is_first=is_first):
-                message(out1 if is_first else out2, not is_even)
-                message(out2 if is_first else out1, is_even)
-
-
-def mid_kernel(own_f, own_c, r1, r2, out2, out1, halo):
+    @pl.when(even)
+    def _():
+        message(inner, True)
+        message(outer, False)
+
+    @pl.when(jnp.logical_not(even))
+    def _():
+        message(inner, False)
+        message(outer, True)
+
+
+def mid_kernel(own_f, own_c, before, both, after, out2, out1, halo):
     gx, gy = lax.axis_index("gx"), lax.axis_index("gy")
     even_x = lax.rem(gx, 2) == 0
     even_y = lax.rem(gy, 2) == 0
-    left_first = even_x == far_first(gy)
-
-    @pl.when(left_first)
-    def _():
-        halo[0] = r1[...]
-        halo[1] = r2[...]
-
-    @pl.when(jnp.logical_not(left_first))
-    def _():
-        halo[0] = r2[...]
-        halo[1] = r1[...]
+    even_side = jnp.where(even_x, 1, 0)
+
+    @pl.when(inner_before(gx, gy))
+    def _():
+        halo[even_side] = before[...]
+
+    @pl.when(jnp.logical_not(inner_before(gx, gy)))
+    def _():
+        halo[even_side] = after[...]
+
+    at_end = jnp.logical_or(gx == 0, gx == lax.axis_size("gx") - 1)
+
+    @pl.when(at_end)
+    def _():
+        halo[1 - even_side] = jnp.zeros((X_ROWS, LANES), F32)
+
+    @pl.when(jnp.logical_and(even_x, jnp.logical_not(at_end)))
+    def _():
+        halo[0] = both[0:X_ROWS]
+
+    @pl.when(jnp.logical_not(jnp.logical_or(even_x, at_end)))
+    def _():
+        halo[1] = both[X_ROWS : 2 * X_ROWS]
 
     def message(out, up):
         for key, (at, rows) in Y_AT.items():
@@ -187,18 +200,23 @@
     gx, gy = lax.axis_index("gx"), lax.axis_index("gy")
     even_y = lax.rem(gy, 2) == 0
 
-    def sides(halo, first, second, even):
-        @pl.when(even)
-        def _():
-            halo[0] = second[...]
-            halo[1] = first[...]
-
-        @pl.when(jnp.logical_not(even))
-        def _():
-            halo[0] = first[...]
-            halo[1] = second[...]
-
-    sides(hy, y1, y2, even_y)
+    @pl.when(even_y)
+    def _():
+        hy[0] = y2[0:Y_ROWS]
+        hy[1] = y1[Y_ROWS : 2 * Y_ROWS]
+
+    @pl.when(jnp.logical_not(even_y))
+    def _():
+        hy[0] = y1[0:Y_ROWS]
+        hy[1] = y2[Y_ROWS : 2 * Y_ROWS]
+
+    @pl.when(gy == 0)
+    def _():
+        hy[0] = jnp.zeros((Y_ROWS, LANES), F32)
+
+    @pl.when(gy == lax.axis_size("gy") - 1)
+    def _():
+        hy[1] = jnp.zeros((Y_ROWS, LANES), F32)
 
     index = {}
 
@@ -338,25 +356,36 @@
 SCRATCH = 3 * (10 + 6 + 6 + 4)
 
 
-def far_first(gy):
-    return gy < -(-5 * lax.axis_size("gy") // 8)
-
-
-def x_exchange(first, second):
+SEAM = 12
+
+
+def inner_before(gx, gy):
+    at = gx % SEAM
+    early = (at == 0) | (at == 1) | (at == 2) | (at == 3) | (at == 6) | (at == 7)
+    return early | (gy >= -(-5 * lax.axis_size("gy") // 8))
+
+
+def x_inner(value, before):
+    ny = lax.axis_size("gy")
+    pairs = []
+    for i in range(0, lax.axis_size("gx") - 1, 2):
+        for j in range(ny):
+            if bool(inner_before(i, j)) == before:
+                pairs += [(i * ny + j, (i + 1) * ny + j), ((i + 1) * ny + j, i * ny + j)]
+    return lax.ppermute(value, ("gx", "gy"), pairs)
+
+
+def gather_pairs(value, axis, first):
     nx, ny = lax.axis_size("gx"), lax.axis_size("gy")
-    pairs = [[], []]
-    for i in range(nx - 1):
-        for j in range(ny):
-            turn = 0 if (i % 2 == 1) == far_first(j) else 1
-            pairs[turn] += [(i * ny + j, (i + 1) * ny + j), ((i + 1) * ny + j, i * ny + j)]
-    return [lax.ppermute(v, ("gx", "gy"), p) for v, p in zip((first, second), pairs)]
-
-
-def swap(value, axis, first):
-    pairs = []
-    for i in range(first, lax.axis_size(axis) - 1, 2):
-        pairs += [(i, i + 1), (i + 1, i)]
-    return lax.ppermute(value, axis, pairs)
+    size, other = (nx, ny) if axis == "gx" else (ny, nx)
+
+    def flat(i, k):
+        return i * ny + k if axis == "gx" else k * ny + i
+
+    groups = [[flat(i, k), flat(i + 1, k)] for k in range(other) for i in range(first, size - 1, 2)]
+    if first:
+        groups += [[flat(i, k), flat(i, k + 1)] for i in (0, size - 1) for k in range(0, other, 2)]
+    return lax.all_gather(value, ("gx", "gy"), axis_index_groups=sorted(groups), tiled=True)
 
 
 def call(kernel, shapes, scratch=(), first=False, last=False):
@@ -395,17 +424,18 @@
     omega_f,
     stretch_f,
 ):
-    out1, out2, own_f, own_c = call(
+    inner, outer, own_f, own_c = call(
         pre_kernel, [(X_ROWS, LANES)] * 2 + [(36, 8, LANES), (16, 4, LANES)], first=True
     )(
         u_now_c, u_prev_c, memory_c, mu_c, lam_c, rho_c, q_c, omega_c,
         u_now_f, u_prev_f, memory_f, mu_f, lam_f, rho_f, q_f, omega_f, stretch_f,
     )
-    out2, out1, halo = call(mid_kernel, [(Y_ROWS, LANES)] * 2 + [(2, X_ROWS, LANES)])(
-        own_f, own_c, *x_exchange(out1, out2)
-    )
-    y2 = swap(out2, "gy", 1)
-    y1 = swap(out1, "gy", 0)
+    before, outer = lax.optimization_barrier((x_inner(inner, True), outer))
+    both, inner = lax.optimization_barrier((gather_pairs(outer, "gx", 1), inner))
+    after = x_inner(inner, False)
+    out2, out1, halo = call(mid_kernel, [(Y_ROWS, LANES)] * 2 + [(2, X_ROWS, LANES)])(own_f, own_c, before, both, after)
+    y2, out1 = lax.optimization_barrier((gather_pairs(out2, "gy", 1), out1))
+    y1 = gather_pairs(out1, "gy", 0)
     return tuple(
         call(
             post_kernel,

time: 34.6 us -> 34.6 us (level)
  the two profiles are of different devices: /device:TPU:57 before, /device:TPU:185 now
where the time goes in v7:
time: 34.6 us; the launch traced here: 34.4 us
  blocking collectives  25.1 us (73%)
  starting transfers between devices  3.79 us (11%)
  Pallas kernels  2.77 us (8%)
  waiting for transfers between devices  1.95 us (6%)
  between operations  0.75 us (2%)
    all_gather x3, blocking collectives, gather_pairs(): lax.all_gather(value, ('gx', 'gy'), axis_index_groups=sorted(groups), til...  25.1 us
    ppermute x2, starting transfers between devices, x_inner(): return lax.ppermute(value, ('gx', 'gy'), pairs)  3.79 us
    pallas_call x3, Pallas kernels, run(): pl.pallas_call(kernel, out_shape=[(jax.ShapeDtypeStruct if last else pltp...  2.77 us
    ppermute x2, waiting for transfers between devices, x_inner(): return lax.ppermute(value, ('gx', 'gy'), pairs)  1.95 us
  transfers between devices with their start and end apart: 2, of which 1 were waited for; matrix products, arithmetic and copies ran while one was open for 0% of the time, Pallas kernels for 0%

profile of v7, /device:TPU:185, one launch (start us, length us, event | category | flops | bytes accessed | tf_op | source)
XLA Modules:
  0.0 34.4 jit_solution(740985942600743193)
XLA Ops:
  0.6 1.3 %shard_map.192 = (f32[144,128]{1,0:T(8,128)S(1)}, f32[144,128]{1,0:T(8,128)S(1)}, f32[36,8,128]{2,1,0:T(8,128)S(1)}, f32[16,4,128]{2,1,0:T(4,128)S(1)}) custom-call(f32[3,2,4,128]{3,2,1,0:T(4,128)} %uc.3, f32[3,2,4,128]{3,2,1,0:T(4,128)} %pc.1, f32[3,3,2,4,128]{4,3,2,1,0:T(4,128)} %mc.3, f32[2,4,128]{2,1,0:T(4,128)} %muc.1, f32[2,4,128]{2,1,0:T(4,128)} %lamc.1, ...), custom_call_target="tpu_custom_call" | custom-call | tf_op jit(solution)/shard_map/pallas_call | solution.py:397
  1.9 3.1 %collective-permute-start = (f32[144,128]{1,0:T(8,128)S(1)}, f32[144,128]{1,0:T(8,128)S(1)}, u32[]{:S(2)}, u32[]{:S(2)}) collective-permute-start(f32[144,128]{1,0:T(8,128)S(1)} %get-tuple-element.24), channel_id=1, source_target_pairs={{0,8},{8,0},{1,9},{9,1},{2,10},{10,2},{3,11},{11,3},{4,12},{12,4},... | collective-permute-start | bytes 221192 | tf_op jit(solution)/shard_map/ppermute | solution.py:375
  5.1 2.0 %collective-permute-done.before = f32[144,128]{1,0:T(8,128)S(1)} collective-permute-done((f32[144,128]{1,0:T(8,128)S(1)}, f32[144,128]{1,0:T(8,128)S(1)}, u32[]{:S(2)}, u32[]{:S(2)}) %collective-permute-start) | collective-permute-done | bytes 73760 | tf_op jit(solution)/shard_map/ppermute | solution.py:375
  7.0 16.0 %all_gather.9.both = f32[288,128]{1,0:T(8,128)S(1)} all-gather(f32[144,128]{1,0:T(8,128)S(1)} %get-tuple-element.22), channel_id=1, replica_groups={{0,1},{2,3},{4,5},{6,7},{8,16},{9,17},{10,18},{11,19},{12,20},{13,21},{..., dimensions={0}, use_global_device_ids=true | all-gather | bytes 221184 | tf_op jit(solution)/shard_map/all_gather | solution.py:388
  23.1 0.7 %collective-permute-start.1 = (f32[144,128]{1,0:T(8,128)S(1)}, f32[144,128]{1,0:T(8,128)S(1)}, u32[]{:S(2)}, u32[]{:S(2)}) collective-permute-start(f32[144,128]{1,0:T(8,128)S(1)} %get-tuple-element.24), channel_id=1, source_target_pairs={{32,40},{40,32},{33,41},{41,33},{34,42},{42,34},{35,43},{43,35},{3... | collective-permute-start | bytes 221192 | tf_op jit(solution)/shard_map/ppermute | solution.py:375
  23.7 0.0 collective-permute-done.1.after
  23.7 0.1 shard_map.193
  23.9 7.0 %all_gather.10.y2 = f32[496,128]{1,0:T(8,128)S(1)} all-gather(f32[248,128]{1,0:T(8,128)S(1)} %get-tuple-element.26), channel_id=1, replica_groups={{0,8},{1,2},{3,4},{5,6},{7,15},{9,10},{11,12},{13,14},{16,24},{17,18},{..., dimensions={0}, use_global_device_ids=true | all-gather | bytes 380928 | tf_op jit(solution)/shard_map/all_gather | solution.py:388
  30.8 0.0 copy-start
  30.8 0.0 copy-start.1
  30.8 0.0 copy-start.2
  30.8 0.0 copy-start.3
  30.8 0.0 copy-start.4
  30.9 0.0 copy-start.5
  30.9 0.0 copy-start.6
  30.9 0.0 copy-start.7
  30.9 2.1 %all_gather.11.y1 = f32[496,128]{1,0:T(8,128)S(1)} all-gather(f32[248,128]{1,0:T(8,128)S(1)} %get-tuple-element.29), channel_id=1, replica_groups={{0,1},{2,3},{4,5},{6,7},{8,9},{10,11},{12,13},{14,15},{16,17},{18,19},{..., dimensions={0}, use_global_device_ids=true | all-gather | bytes 380928 | tf_op jit(solution)/shard_map/all_gather | solution.py:388
  33.0 0.0 copy-done
  33.0 0.0 copy-done.1
  33.0 0.0 copy-done.2
  33.0 0.0 copy-done.3
  33.0 0.0 copy-done.4
  33.0 0.0 copy-done.5
  33.1 0.0 copy-done.6
  33.1 0.0 copy-done.7
  33.1 1.3 %shard_map.194 = (f32[3,2,4,128]{3,2,1,0:T(4,128)}, f32[3,4,8,128]{3,2,1,0:T(8,128)}, f32[3,3,2,4,128]{4,3,2,1,0:T(4,128)}, f32[3,3,4,8,128]{4,3,2,1,0:T(8,128)}) custom-call(f32[36,8,128]{2,1,0:T(8,128)S(1)} %get-tuple-element.17.own_f, f32[16,4,128]{2,1,0:T(4,128)S(1)} %get-tuple-element.18.own_c, f32[2,144,128]{2,1,0:T(8,128)S(1)} %get-tuple-element.25.hx, ...), custom_call_target="tpu_custom_call" | custom-call | tf_op jit(solution)/shard_map/pallas_call | solution.py:397
Async XLA Ops:
  1.9 5.1 %collective-permute-start = (f32[144,128]{1,0:T(8,128)S(1)}, f32[144,128]{1,0:T(8,128)S(1)}, u32[]{:S(2)}, u32[]{:S(2)}) collective-permute-start(f32[144,128]{1,0:T(8,128)S(1)} %get-tuple-element.24), channel_id=1, source_target_pairs={{0,8},{8,0},{1,9},{9,1},{2,10},{10,2},{3,11},{11,3},{4,12},{12,4},... | collective-permute-start | bytes 221192 | tf_op jit(solution)/shard_map/ppermute | solution.py:375
  23.1 0.7 %collective-permute-start.1 = (f32[144,128]{1,0:T(8,128)S(1)}, f32[144,128]{1,0:T(8,128)S(1)}, u32[]{:S(2)}, u32[]{:S(2)}) collective-permute-start(f32[144,128]{1,0:T(8,128)S(1)} %get-tuple-element.24), channel_id=1, source_target_pairs={{32,40},{40,32},{33,41},{41,33},{34,42},{42,34},{35,43},{43,35},{3... | collective-permute-start | bytes 221192 | tf_op jit(solution)/shard_map/ppermute | solution.py:375
  30.8 2.2 %copy-start = (f32[3,3,4,8,128]{4,3,2,1,0:T(8,128)S(1)}, f32[3,3,4,8,128]{4,3,2,1,0:T(8,128)}, u32[]{:S(2)}) copy-start(f32[3,3,4,8,128]{4,3,2,1,0:T(8,128)} %mf.3) | copy-start | bytes 442372
  30.8 2.2 %copy-start.1 = (f32[3,4,8,128]{3,2,1,0:T(8,128)S(1)}, f32[3,4,8,128]{3,2,1,0:T(8,128)}, u32[]{:S(2)}) copy-start(f32[3,4,8,128]{3,2,1,0:T(8,128)} %uf.3) | copy-start | bytes 147460
  30.8 2.2 %copy-start.2 = (f32[3,4,8,128]{3,2,1,0:T(8,128)S(1)}, f32[3,4,8,128]{3,2,1,0:T(8,128)}, u32[]{:S(2)}) copy-start(f32[3,4,8,128]{3,2,1,0:T(8,128)} %qf.3) | copy-start | bytes 147460
  30.8 2.2 %copy-start.3 = (f32[3,4,8,128]{3,2,1,0:T(8,128)S(1)}, f32[3,4,8,128]{3,2,1,0:T(8,128)}, u32[]{:S(2)}) copy-start(f32[3,4,8,128]{3,2,1,0:T(8,128)} %omf.3) | copy-start | bytes 147460
  30.8 2.2 %copy-start.4 = (f32[3,3,2,4,128]{4,3,2,1,0:T(4,128)S(1)}, f32[3,3,2,4,128]{4,3,2,1,0:T(4,128)}, u32[]{:S(2)}) copy-start(f32[3,3,2,4,128]{4,3,2,1,0:T(4,128)} %mc.3) | copy-start | bytes 110596
  30.9 2.2 %copy-start.5 = (f32[3,2,4,128]{3,2,1,0:T(4,128)S(1)}, f32[3,2,4,128]{3,2,1,0:T(4,128)}, u32[]{:S(2)}) copy-start(f32[3,2,4,128]{3,2,1,0:T(4,128)} %uc.3) | copy-start | bytes 36868
  30.9 2.2 %copy-start.6 = (f32[3,2,4,128]{3,2,1,0:T(4,128)S(1)}, f32[3,2,4,128]{3,2,1,0:T(4,128)}, u32[]{:S(2)}) copy-start(f32[3,2,4,128]{3,2,1,0:T(4,128)} %qc.3) | copy-start | bytes 36868
  30.9 2.2 %copy-start.7 = (f32[3,2,4,128]{3,2,1,0:T(4,128)S(1)}, f32[3,2,4,128]{3,2,1,0:T(4,128)}, u32[]{:S(2)}) copy-start(f32[3,2,4,128]{3,2,1,0:T(4,128)} %omc.3) | copy-start | bytes 36868
